TPU v7x, 256 devices: a whole 4x4x8 slice. The times are simulated.
256 devices in a mesh: expert: 8 (over x, core), dp: 32 (over y, z).
Axes of the slice: x: 4, y: 4, z: 8, core: 2. Of those that a mesh axis runs over, the one named last changes fastest.
Arguments:
- tokens: bfloat16 [32768, 1024], P(('expert', 'dp')), may hold values from -6 to 6
- norm_gain: float32 [1024], replicated, may hold values from 0.1 to 1.9
- router_weight: bfloat16 [1024, 8], replicated, may hold values from -0.3984375 to 0.3984375
- shared_gate_vector: float32 [1024], replicated, may hold values from -0.4 to 0.4
- expert_ids: int32 [32768, 2], P(('expert', 'dp')), may hold values from 0 to 7, all different within a row; in each aligned block of 128 rows (0 to 127, 128 to 255, ...) at most 48 rows name the same one
- gate_weight: bfloat16 [8, 1024, 4096], P('expert', None, 'dp'), may hold values from -0.1875 to 0.1875
- up_weight: bfloat16 [8, 1024, 4096], P('expert', None, 'dp'), may hold values from -0.1875 to 0.1875
- down_weight: bfloat16 [8, 1024, 4096], P('expert', None, 'dp'), may hold values from -0.09375 to 0.09375
- shared_gate_weight: bfloat16 [1024, 4096], P(None, 'expert'), may hold values from -0.1875 to 0.1875
- shared_up_weight: bfloat16 [1024, 4096], P(None, 'expert'), may hold values from -0.1875 to 0.1875
- shared_down_weight: bfloat16 [4096, 1024], P('expert'), may hold values from -0.09375 to 0.09375
Outputs:
- mixed: bfloat16 [32768, 1024], P(('expert', 'dp'))
Inputs may be any that keep to these rules, and one draw needn't show every extreme that they name: `expert_ids`: in each aligned block of 128 rows (the rows of one device) no expert is named by more than 48 pairs, and in some block one expert is named by exactly 48; the two ids of a row differ.
All inputs are finite; a program needn't handle non-finite values.
Results may differ from a plain program's by a relative error of at most 0.0085.
Values may be sent and summed in bfloat16 or wider, within the bound.
A program may use at most 128 MiB of HBM per device.

v0:
```python
import jax
import jax.numpy as jnp
from jax import lax
from jax.sharding import PartitionSpec as P


def from_everyone(array, axis):
    size = lax.axis_size(axis)
    return lax.all_to_all(
        jnp.broadcast_to(array[None], (size, *array.shape)), axis, 0, 0, tiled=True
    )


def laid_out(pieces, dim):
    pieces = jnp.moveaxis(pieces, 0, dim)
    lengths = pieces.shape
    return pieces.reshape(*lengths[:dim], lengths[dim] * lengths[dim + 1], *lengths[dim + 2 :])


def gathered_copies(array, axis, dim):
    pieces = from_everyone(array, axis)
    return laid_out(pieces, dim)


def in_blocks(array, dim, size):
    before, after = (array.shape[:dim], array.shape[dim + 1 :])
    return jnp.moveaxis(array.reshape(*before, size, -1, *after), dim, 0)


def summed_on_arrival(array, axis, dim):
    size = lax.axis_size(axis)
    pieces = lax.all_to_all(in_blocks(array, dim, size), axis, 0, 0, tiled=True)
    return jnp.sum(pieces.astype(jnp.float32), axis=0)


def sent_together(arrays, axis, dim, along):
    ends, at = ([], 0)
    for a in arrays[:-1]:
        at += a.shape[along]
        ends.append(at)
    both = jnp.concatenate(arrays, axis=along)
    return tuple(jnp.split(lax.all_gather(both, axis, axis=dim, tiled=True), ends, axis=along))


def rms_norm(values, gain):
    floats = values.astype(jnp.float32)
    mean_square = jnp.mean(floats * floats, axis=-1, keepdims=True)
    return (floats * lax.rsqrt(mean_square + 1e-06) * gain).astype(jnp.bfloat16)


def routing(normed, router_weight, expert_ids):
    logits = jnp.dot(normed, router_weight, preferred_element_type=jnp.float32)
    onehot = (
        expert_ids[:, :, None] == jnp.arange(router_weight.shape[1], dtype=jnp.int32)[None, None, :]
    )
    picked = jnp.sum(jnp.where(onehot, logits[:, None, :], jnp.float32(0.0)), axis=-1)
    first_weight = jax.nn.sigmoid(picked[:, 0] - picked[:, 1])
    return jnp.stack([first_weight, 1.0 - first_weight], axis=1)


def slot_of(block_ids, experts):
    flat_ids = block_ids.reshape(-1)
    onehot = (flat_ids[:, None] == jnp.arange(experts, dtype=jnp.int32)[None, :]).astype(jnp.int32)
    before = jnp.cumsum(onehot, axis=0) - onehot
    return jnp.sum(before * onehot, axis=1).reshape(block_ids.shape)


def swiglu_hidden(inputs, gate_piece, up_piece):
    gate_part = jnp.dot(inputs, gate_piece, preferred_element_type=jnp.float32)
    up_part = jnp.dot(inputs, up_piece, preferred_element_type=jnp.float32)
    return (jax.nn.silu(gate_part) * up_part).astype(jnp.bfloat16)


def down_product(hidden, down_piece):
    return lax.dot_general(
        hidden, down_piece, (((1,), (1,)), ((), ())), preferred_element_type=jnp.float32
    )


def body(
    tokens,
    norm_gain,
    router_weight,
    shared_gate_vector,
    expert_ids,
    gate_weight,
    up_weight,
    down_weight,
    shared_gate_weight,
    shared_up_weight,
    shared_down_weight,
):
    experts = lax.axis_size("expert")
    tok_rows = tokens.shape[0]
    width = tokens.shape[1]
    capacity = 3 * tok_rows // experts
    normed = rms_norm(tokens, norm_gain)
    route_weight = routing(normed, router_weight, expert_ids)
    slot = slot_of(expert_ids, experts)
    target = expert_ids * capacity + slot
    slot_iota = jnp.arange(experts * capacity, dtype=jnp.int32)[:, None]
    dispatch_table = (
        (target[:, 0][None, :] == slot_iota) | (target[:, 1][None, :] == slot_iota)
    ).astype(jnp.bfloat16)
    outgoing = jnp.dot(dispatch_table, normed, preferred_element_type=jnp.float32).astype(
        jnp.bfloat16
    )
    outgoing = outgoing.reshape(experts, capacity, width)
    arrived = lax.all_to_all(outgoing, "expert", split_axis=0, concat_axis=0, tiled=True).reshape(
        experts * capacity, width
    )
    pieces = sent_together((gate_weight, up_weight, down_weight), "dp", 2, 0)
    hidden = swiglu_hidden(arrived, pieces[0][0], pieces[1][0])
    expert_out = down_product(hidden, pieces[2][0])
    expert_out = expert_out.astype(jnp.bfloat16).reshape(experts, capacity, width)
    returned_rows = lax.all_to_all(
        expert_out, "expert", split_axis=0, concat_axis=0, tiled=True
    ).reshape(experts * capacity, width)
    fetched = returned_rows[target].astype(jnp.float32)
    routed = jnp.sum(route_weight[:, :, None] * fetched, axis=1)
    gathered = gathered_copies(normed, "expert", 0)
    hidden = swiglu_hidden(gathered, shared_gate_weight, shared_up_weight)
    shared = summed_on_arrival(
        jnp.dot(hidden, shared_down_weight, preferred_element_type=jnp.float32).astype(
            jnp.bfloat16
        ),
        "expert",
        0,
    )
    shared_gate = jax.nn.sigmoid(jnp.sum(normed.astype(jnp.float32) * shared_gate_vector, axis=-1))
    return (routed + shared_gate[:, None] * shared).astype(jnp.bfloat16)


def solution(mesh):
    return jax.shard_map(
        body,
        mesh=mesh,
        in_specs=(
            P(("expert", "dp"), None),
            P(),
            P(),
            P(),
            P(("expert", "dp"), None),
            P("expert", None, "dp"),
            P("expert", None, "dp"),
            P("expert", None, "dp"),
            P(None, "expert"),
            P(None, "expert"),
            P("expert", None),
        ),
        out_specs=P(("expert", "dp"), None),
        check_vma=False,
    )
```

profile of v0, /device:TPU:4, one launch (start us, length us, event | category | flops | bytes accessed | tf_op | source)
XLA Modules:
  0.0 261.5 jit_solution(6149935465993720360)
XLA Ops:
  6.5 2.2 pad_maximum_fusion
  8.7 1.1 fusion.5
  9.8 1.2 multiply_reduce_fusion.1
  11.1 1.7 broadcast_in_dim.19
  12.7 5.7 %all-to-all-start.2 = ((bf16[8,128,1024]{2,1,0:T(8,128)(2,1)}), bf16[8,128,1024]{2,1,0:T(8,128)(2,1)S(1)}, u32[]{:S(2)}, u32[]{:S(2)}) async-start(bf16[8,128,1024]{2,1,0:T(8,128)(2,1)} %broadcast_in_dim.19), calls=%async_computation.2 | async-start | bytes 4194304 | tf_op jit(solution)/shard_map/all_to_all | solution.py:9
  18.9 0.6 reduce-window.6
  20.3 1.2 convolution_convert_fusion.1
  21.5 21.0 %all-to-all-done.2 = bf16[8,128,1024]{2,1,0:T(8,128)(2,1)S(1)} async-done(((bf16[8,128,1024]{2,1,0:T(8,128)(2,1)}), bf16[8,128,1024]{2,1,0:T(8,128)(2,1)S(1)}, u32[]{:S(2)}, u32[]{:S(2)}) %all-to-all-start.2) | async-done | bytes 2097184 | tf_op jit(solution)/shard_map/all_to_all | solution.py:9
  42.5 7.3 %all-to-all-start = ((bf16[8,48,1024]{2,1,0:T(8,128)(2,1)}), bf16[8,48,1024]{2,1,0:T(8,128)(2,1)}, u32[]{:S(2)}, u32[]{:S(2)}) async-start(bf16[8,48,1024]{2,1,0:T(8,128)(2,1)} %bitcast.4), calls=%async_computation | async-start | bytes 1572864 | tf_op jit(solution)/shard_map/all_to_all | solution.py:109
  49.7 3.9 %fusion.19 = f32[1024,512]{1,0:T(8,128)} fusion(bf16[1024,1024]{1,0:T(8,128)(2,1)S(1)} %bitcast.46, bf16[1024,512]{1,0:T(8,128)(2,1)} %param.19), kind=kOutput, calls=%fused_computation.50 | convolution fusion | flops 1073741824 | bytes 5242880 | tf_op jit(solution)/shard_map/dot_general | solution.py:69
  53.6 5.7 %convolution_convert_fusion = bf16[1024,1024]{1,0:T(8,128)(2,1)} fusion(bf16[512,1024]{1,0:T(8,128)(2,1)S(1)} %copy-done, f32[1024,512]{1,0:T(8,128)} %fusion.19, bf16[1024,1024]{1,0:T(8,128)(2,1)S(1)} %bitcast.47, bf16[1024,512]{1,0:T(8,128)(2,1)} %param.20), kind=kOutput, calls=%fused_computation.10 | convolution fusion | flops 2151677952 | bytes 8388608 | tf_op jit(solution)/shard_map/dot_general | solution.py:124
  59.3 0.5 all-to-all-done
  59.8 6.7 %all-to-all-start.3 = ((bf16[8,128,1024]{2,1,0:T(8,128)(2,1)}), bf16[8,128,1024]{2,1,0:T(8,128)(2,1)S(1)}, u32[]{:S(2)}, u32[]{:S(2)}) async-start(bf16[8,128,1024]{2,1,0:T(8,128)(2,1)} %bitcast.48), calls=%async_computation.3 | async-start | bytes 4194304 | tf_op jit(solution)/shard_map/all_to_all | solution.py:32
  66.5 142.7 %all-gather.2.cloned.1.call-done = bf16[3,1024,4096]{2,1,0:T(8,128)(2,1)} async-done(((bf16[3,1024,128]{2,1,0:T(8,128)(2,1)}), bf16[3,1024,4096]{2,1,0:T(8,128)(2,1)}) %all-gather.2.cloned.1.call-update) | async-done | bytes 25165840 | tf_op jit(solution)/shard_map/all_gather | solution.py:42
  209.2 9.8 %fusion.2 = f32[384,4096]{1,0:T(8,128)} fusion(bf16[384,1024]{1,0:T(8,128)(2,1)} %bitcast.5, bf16[3,1024,4096]{2,1,0:T(8,128)(2,1)} %all-gather.2.cloned.1.call-done), kind=kOutput, calls=%fused_computation.6 | convolution fusion | flops 3221225472 | bytes 15466496 | tf_op jit(solution)/shard_map/dot_general | solution.py:69
  218.9 15.6 %fusion.3 = bf16[384,1024]{1,0:T(8,128)(2,1)} fusion(bf16[3,1024,4096]{2,1,0:T(8,128)(2,1)} %all-gather.2.cloned.1.call-done, f32[384,4096]{1,0:T(8,128)} %fusion.2, bf16[384,1024]{1,0:T(8,128)(2,1)} %bitcast.5), kind=kOutput, calls=%fused_computation.12 | convolution fusion | flops 6452281344 | bytes 24641536 | tf_op jit(solution)/shard_map/dot_general | solution.py:75
  234.5 1.4 copy-done.1
  235.9 4.8 %all-to-all-start.1 = ((bf16[8,48,1024]{2,1,0:T(8,128)(2,1)}), bf16[8,48,1024]{2,1,0:T(8,128)(2,1)S(1)}, u32[]{:S(2)}, u32[]{:S(2)}) async-start(bf16[8,48,1024]{2,1,0:T(8,128)(2,1)} %bitcast.49), calls=%async_computation.1 | async-start | bytes 1572864 | tf_op jit(solution)/shard_map/all_to_all | solution.py:116
  241.1 2.0 convert_reduce_fusion
  243.1 7.6 %all-to-all-done.1 = bf16[8,48,1024]{2,1,0:T(8,128)(2,1)S(1)} async-done(((bf16[8,48,1024]{2,1,0:T(8,128)(2,1)}), bf16[8,48,1024]{2,1,0:T(8,128)(2,1)S(1)}, u32[]{:S(2)}, u32[]{:S(2)}) %all-to-all-start.1) | async-done | bytes 786464 | tf_op jit(solution)/shard_map/all_to_all | solution.py:116
  250.7 1.2 gather_fusion
  251.8 0.7 reshape.78
  252.5 1.3 multiply_reduce_fusion
  253.8 0.8 add_convert_fusion
  (32 shorter events, 1.6 us)
Async XLA Ops:
  6.5 47.1 %copy-start = (bf16[512,1024]{1,0:T(8,128)(2,1)S(1)}, bf16[512,1024]{1,0:T(8,128)(2,1)}, u32[]{:S(2)}) copy-start(bf16[512,1024]{1,0:T(8,128)(2,1)} %param.21) | copy-start | bytes 3145732
  6.5 202.6 %all-gather.2.cloned.1.call-start = ((), (), s32[]{:S(2)}) async-start(), calls=%async_computation.4 | async-start | bytes 25952256 | tf_op jit(solution)/shard_map/all_gather | solution.py:42
  11.1 7.4 %copy-start.3 = (s32[128,2]{0,1:T(2,128)S(1)}, s32[128,2]{0,1:T(2,128)}, u32[]{:S(2)}) copy-start(s32[128,2]{0,1:T(2,128)} %param.15) | copy-start | bytes 3076
  11.1 9.0 %copy-start.2 = (bf16[1024,8]{0,1:T(8,128)(2,1)S(1)}, bf16[1024,8]{0,1:T(8,128)(2,1)}, u32[]{:S(2)}) copy-start(bf16[1024,8]{0,1:T(8,128)(2,1)} %param.13) | copy-start | bytes 49156
  12.7 29.8 %all-to-all-start.2 = ((bf16[8,128,1024]{2,1,0:T(8,128)(2,1)}), bf16[8,128,1024]{2,1,0:T(8,128)(2,1)S(1)}, u32[]{:S(2)}, u32[]{:S(2)}) async-start(bf16[8,128,1024]{2,1,0:T(8,128)(2,1)} %broadcast_in_dim.19), calls=%async_computation.2 | async-start | bytes 4194304 | tf_op jit(solution)/shard_map/all_to_all | solution.py:9
  42.5 17.3 %all-to-all-start = ((bf16[8,48,1024]{2,1,0:T(8,128)(2,1)}), bf16[8,48,1024]{2,1,0:T(8,128)(2,1)}, u32[]{:S(2)}, u32[]{:S(2)}) async-start(bf16[8,48,1024]{2,1,0:T(8,128)(2,1)} %bitcast.4), calls=%async_computation | async-start | bytes 1572864 | tf_op jit(solution)/shard_map/all_to_all | solution.py:109
  59.8 174.7 %all-to-all-start.3 = ((bf16[8,128,1024]{2,1,0:T(8,128)(2,1)}), bf16[8,128,1024]{2,1,0:T(8,128)(2,1)S(1)}, u32[]{:S(2)}, u32[]{:S(2)}) async-start(bf16[8,128,1024]{2,1,0:T(8,128)(2,1)} %bitcast.48), calls=%async_computation.3 | async-start | bytes 4194304 | tf_op jit(solution)/shard_map/all_to_all | solution.py:32
  234.5 1.4 copy-start.1
  235.9 14.8 %all-to-all-start.1 = ((bf16[8,48,1024]{2,1,0:T(8,128)(2,1)}), bf16[8,48,1024]{2,1,0:T(8,128)(2,1)S(1)}, u32[]{:S(2)}, u32[]{:S(2)}) async-start(bf16[8,48,1024]{2,1,0:T(8,128)(2,1)} %bitcast.49), calls=%async_computation.1 | async-start | bytes 1572864 | tf_op jit(solution)/shard_map/all_to_all | solution.py:116
Sparse Core Ops, SparseCore 0:
  9.8 199.3 all-gather.1
where the time goes:
time: 265 us; the launch traced here: 262 us
  waiting for transfers between devices  172 us (65%)
  matrix products  36.4 us (14%)
  starting transfers between devices  24.5 us (9%)
  between operations  13.5 us (5%)
  other arithmetic  9.47 us (4%)
  local copies, waits for them, and re-layouts  6.03 us (2%)
    all_gather x1, waiting for transfers between devices, sent_together(): lax.all_gather(both, axis, axis=dim, tiled=True)  143 us
    all_to_all x1, waiting for transfers between devices, from_everyone(): lax.all_to_all(jnp.broadcast_to(array[None], (size, *array.shape)), axis,...  21 us
    dot_general x1, matrix products, down_product(): lax.dot_general(hidden, down_piece, (((1,), (1,)), ((), ())), preferred_e...  15.6 us
    dot_general x2, matrix products, swiglu_hidden(): gate_part = jnp.dot(inputs, gate_piece, preferred_element_type=jnp.float32)  13.7 us
    all_to_all x1, waiting for transfers between devices, body(): lax.all_to_all(expert_out, 'expert', split_axis=0, concat_axis=0, tiled=T...  7.56 us
    all_to_all x1, starting transfers between devices, body(): lax.all_to_all(outgoing, 'expert', split_axis=0, concat_axis=0, tiled=True)  7.26 us
    all_to_all x1, starting transfers between devices, summed_on_arrival(): pieces = lax.all_to_all(in_blocks(array, dim, size), axis, 0, 0, tiled=True)  6.69 us
    all_to_all x1, starting transfers between devices, from_everyone(): lax.all_to_all(jnp.broadcast_to(array[None], (size, *array.shape)), axis,...  5.74 us
  transfers between devices with their start and end apart: 5, of which 4 were waited for; matrix products, arithmetic and copies ran while one was open for 17% of the time, Pallas kernels for 0%

commit v1 on v0

v1 whole, which is shorter than its diff:
```python
import jax
import jax.numpy as jnp
from jax import lax
from jax.experimental import pallas as pl
from jax.experimental.pallas import tpu as pltpu
from jax.sharding import PartitionSpec as P

MESH = pl.DeviceIdType.MESH
BF16 = jnp.bfloat16
F32 = jnp.float32

XN, CN, YN, ZN = 4, 2, 4, 8
TOK = 128
D = 1024
HID = 128
SHID = 512
CAP = 48
BLOCKS = XN * CN
ROWS = BLOCKS * CAP
NC = 4
CW = D // NC
HALF_R = ROWS // 2
HALF_T = TOK // 2
COPIES = 256

NT = (((1,), (1,)), ((), ()))


def dot(a, b):
    return jnp.dot(a, b, preferred_element_type=F32)


class Links:
    def __init__(self, send_sem, recv_sem):
        self.send_sem, self.recv_sem = send_sem, recv_sem
        self.copies, self.started, self.arrived = {}, [], set()

    def add(self, name, src, dst, device):
        k = len(self.copies)
        self.copies[name] = pltpu.make_async_remote_copy(
            src_ref=src,
            dst_ref=dst,
            send_sem=self.send_sem.at[k],
            recv_sem=self.recv_sem.at[k],
            device_id=device,
            device_id_type=MESH,
        )

    def send(self, *name):
        self.copies[name].start()
        self.started.append(name)

    def arrive(self, *name):
        if name not in self.arrived:
            self.arrived.add(name)
            self.copies[name].wait_recv()

    def finish(self):
        assert set(self.started) == set(self.copies) == self.arrived
        for name in self.started:
            self.copies[name].wait_send()


def silu_mul(g, u):
    return (g * jax.nn.sigmoid(g) * u).astype(BF16)


def layer_kernel(
    tokens, ids, gain, router, gate_vector, gate, up, down, sgate, sup, sdown, out,
    tok, idt, xn, sel, wcol, gcol, rows, gu, dn, hid, sgw, suw, sdw, shared,
    yown, ymerge, ys1, ys2, ys3, yr1, yr2, yr3,
    cown, csend, crecv, xmerge, xs1, xs2, xs3, xr1, xr2, xr3,
    local_sem, send_sem, recv_sem,
):
    e, d = lax.axis_index("expert"), lax.axis_index("dp")
    x, core = lax.div(e, CN), lax.rem(e, CN)
    y, z = lax.div(d, ZN), lax.rem(d, ZN)

    def step_x(by):
        return (lax.rem(x + by, XN) * CN + core, d)

    def step_y(by):
        return (e, lax.rem(y + by, YN) * ZN + z)

    def step_z(by):
        return (e, y * ZN + lax.rem(z + by, ZN))

    to_x = (step_x(1), step_x(XN - 1))
    to_y = (step_y(1), step_y(YN - 1))
    to_z = (step_z(1), step_z(ZN - 1))
    partner = (x * CN + (1 - core), d)

    local = [
        pltpu.make_async_copy(src, dst, local_sem.at[i])
        for i, (src, dst) in enumerate(
            (
                (tokens, tok.at[0, 0]),
                (ids, idt.at[0, 0]),
                (gate, gu.at[0, :, pl.ds(0, HID)]),
                (up, gu.at[0, :, pl.ds(HID, HID)]),
                (sgate, sgw),
                (sup, suw),
                (sdown, sdw),
                (down, dn.at[:, pl.ds(0, HID)]),
            )
        )
    ]
    for copy in local:
        copy.start()

    barrier = pltpu.get_barrier_semaphore()
    for device in (*to_x, *to_y, *to_z, partner):
        pl.semaphore_signal(barrier, inc=1, device_id=device, device_id_type=MESH)
    pl.semaphore_wait(barrier, 7)

    links = Links(send_sem, recv_sem)
    add, send, arrive = links.add, links.send, links.arrive

    near = (1, 3)
    lo, hi = pl.ds(0, HALF_T), pl.ds(HALF_T, HALF_T)
    for way in range(2):
        add(("xt", way), tok.at[0, 0], tok.at[near[way], 0], to_x[way])
        add(("xi", way), idt.at[0, 0], idt.at[near[way], 0], to_x[way])
        part = (lo, hi)[way]
        add(("xf", way), tok.at[near[way], 0, part], tok.at[2, 0, part], to_x[way])
    add(("xif",), idt.at[1, 0], idt.at[2, 0], to_x[0])
    for rx in range(XN):
        add(("ct", rx), tok.at[rx, 0], tok.at[rx, 1], partner)
        add(("ci", rx), idt.at[rx, 0], idt.at[rx, 1], partner)

    for b in range(BLOCKS):
        span = pl.ds(b * CAP, CAP)
        for way in range(2):
            add(("yr", way, b), rows.at[0, span], rows.at[near[way], span], to_y[way])
        way = b % 2
        add(("yf", b), rows.at[near[way], span], rows.at[2, span], to_y[way])

    def z_slot(way, hop):
        return hop if way == 0 else (ZN - hop) % ZN

    lanes = (pl.ds(0, HID), pl.ds(HID, HID))
    for hop in range(1, 5):
        for way in range(2):
            src, dst = z_slot(way, hop - 1), z_slot(way, hop)
            for which in range(2):
                if hop < 4 or which == way:
                    add(("zw", way, hop, which), gu.at[src, :, lanes[which]], gu.at[dst, :, lanes[which]], to_z[way])
            for c in range(NC):
                if hop < 4 or c % 2 == way:
                    span = pl.ds(c * CW, CW)
                    add(
                        ("zd", way, hop, c),
                        dn.at[span, pl.ds(src * HID, HID)],
                        dn.at[span, pl.ds(dst * HID, HID)],
                        to_z[way],
                    )

    for c in range(NC):
        for way in range(2):
            add(("y1", way, c), ys1.at[c, way], yr1.at[c, way], to_y[way])
            add(("y2", way, c), ys2.at[c, way], yr2.at[c, way], to_y[way])
            add(("y3", way, c), ys3.at[c, way], yr3.at[c, way], to_y[way])
            add(("x1", way, c), xs1.at[c, way], xr1.at[c, way], to_x[way])
            add(("x2", way, c), xs2.at[c, way], xr2.at[c, way], to_x[way])
            add(("x3", way, c), xs3.at[c, way], xr3.at[c, way], to_x[way])
        add(("cr", c), csend.at[c], crecv.at[c], partner)
    assert len(links.copies) <= COPIES

    row_iota = lax.broadcasted_iota(jnp.int32, (TOK, TOK), 0)
    lane_iota = lax.broadcasted_iota(jnp.int32, (TOK, TOK), 1)
    eye = jnp.where(row_iota == lane_iota, 1.0, 0.0).astype(BF16)
    earlier = jnp.where(lane_iota < row_iota, 1.0, 0.0).astype(BF16)
    lane = lane_iota.astype(F32)
    lane8 = lax.broadcasted_iota(jnp.int32, (TOK, BLOCKS), 1).astype(F32)
    mine = e.astype(F32)

    def take_block(b):
        rx, cc = b // 2, b % 2
        wide = tok[rx, cc].astype(F32)
        mean_square = jnp.mean(wide * wide, axis=-1, keepdims=True)
        n = (wide * lax.rsqrt(mean_square + 1e-06) * gain[...]).astype(BF16)
        xn[pl.ds(b * TOK, TOK), :] = n
        logits = dot(n, router[...])
        columns = lax.dot_general(eye, idt[rx, cc].astype(BF16), NT, preferred_element_type=F32)
        id0, id1 = columns[:, 0:1], columns[:, 1:2]
        l0 = jnp.sum(jnp.where(lane8 == id0, logits, 0.0), axis=-1, keepdims=True)
        l1 = jnp.sum(jnp.where(lane8 == id1, logits, 0.0), axis=-1, keepdims=True)
        w0 = jax.nn.sigmoid(l0 - l1)
        wcol[b] = jnp.where(id0 == mine, w0, 0.0) + jnp.where(id1 == mine, 1.0 - w0, 0.0)
        named = jnp.where(id0 == mine, 1.0, 0.0) + jnp.where(id1 == mine, 1.0, 0.0)
        named = jnp.broadcast_to(named, (TOK, TOK))
        slot = dot(earlier, named.astype(BF16))
        chosen = jnp.where(slot == lane, named, 0.0)
        sel[b] = chosen.astype(BF16)
        table = jnp.transpose(chosen)[0:CAP, :].astype(BF16)
        rows[0, pl.ds(b * CAP, CAP), :] = dot(table, n).astype(BF16)
        gcol[b] = jax.nn.sigmoid(
            jnp.sum(n.astype(F32) * gate_vector[...], axis=-1, keepdims=True)
        )
        for way in range(2):
            send("yr", way, b)

    def shared_pair(p):
        a = xn[pl.ds(p * 2 * TOK, 2 * TOK), :]
        hidden = silu_mul(dot(a, sgw[...]), dot(a, suw[...]))
        part = dot(hidden, sdw[...])
        for k in range(2):
            b = 2 * p + k
            shared[b] = part[k * TOK : (k + 1) * TOK] * gcol[b]

    def gate_up(s):
        @pl.loop(0, YN)
        def _(r):
            both = dot(rows[r], gu[s])
            hid[r, :, pl.ds(s * HID, HID)] = silu_mul(both[:, :HID], both[:, HID:])

    def down_out(r, c):
        return lax.dot_general(
            hid[r], dn[pl.ds(c * CW, CW), :], NT, preferred_element_type=F32
        )

    def forward_weights(hop, which):
        for way in range(2):
            if ("zw", way, hop, which) in links.copies:
                arrive("zw", way, hop, which)
                if ("zw", way, hop + 1, which) in links.copies:
                    send("zw", way, hop + 1, which)

    def forward_rows(b):
        way = b % 2
        arrive("yr", way, b)
        send("yf", b)

    def down_round(r):
        for hop in range(1, 5):
            c = r - hop + 1
            if 0 <= c < NC:
                for way in range(2):
                    if ("zd", way, hop, c) in links.copies:
                        if hop > 1:
                            arrive("zd", way, hop - 1, c)
                        send("zd", way, hop, c)

    def out_chunk(c):
        for hop in range(1, 5):
            for way in range(2):
                if ("zd", way, hop, c) in links.copies:
                    arrive("zd", way, hop, c)
        far = down_out(2, c)
        ys1[c, 0] = far[:HALF_R].astype(BF16)
        ys1[c, 1] = far[HALF_R:].astype(BF16)
        send("y1", 0, c)
        send("y1", 1, c)
        after = down_out(3, c)
        ys2[c, 0] = after[HALF_R:].astype(BF16)
        send("y2", 0, c)
        ymerge[c, 0] = after[:HALF_R]
        before = down_out(1, c)
        ys2[c, 1] = before[:HALF_R].astype(BF16)
        send("y2", 1, c)
        ymerge[c, 1] = before[HALF_R:]
        yown[c] = down_out(0, c)

    def y_merge(c):
        for way in range(2):
            arrive("y1", way, c)
            ys3[c, way] = (ymerge[c, way] + yr1[c, way].astype(F32)).astype(BF16)
            send("y3", way, c)

    def combine(c):
        for way in range(2):
            arrive("y2", way, c)
        for way in range(2):
            arrive("y3", way, c)
        own = yown[c]
        top = own[:HALF_R] + yr3[c, 0].astype(F32) + yr2[c, 1].astype(F32)
        bottom = own[HALF_R:] + yr2[c, 0].astype(F32) + yr3[c, 1].astype(F32)
        per_half = HALF_R // CAP
        halves = (top.astype(BF16), bottom.astype(BF16))
        for cc in (1, 0):
            for rx in range(XN):
                b = rx * 2 + cc
                k = b % per_half
                chosen = halves[b // per_half][k * CAP : (k + 1) * CAP]
                part = dot(sel[b][:, :CAP], chosen) * wcol[b] + shared[b, :, pl.ds(c * CW, CW)]
                if cc == 1:
                    csend[c, rx] = part.astype(BF16)
                else:
                    cown[c, rx] = part
            if cc == 1:
                send("cr", c)

    def core_merge(c):
        arrive("cr", c)
        far = cown[c, 2] + crecv[c, 2].astype(F32)
        xs1[c, 0] = far[:HALF_T].astype(BF16)
        xs1[c, 1] = far[HALF_T:].astype(BF16)
        send("x1", 0, c)
        send("x1", 1, c)
        after = cown[c, 3] + crecv[c, 3].astype(F32)
        xs2[c, 0] = after[HALF_T:].astype(BF16)
        send("x2", 0, c)
        xmerge[c, 0] = after[:HALF_T]
        before = cown[c, 1] + crecv[c, 1].astype(F32)
        xs2[c, 1] = before[:HALF_T].astype(BF16)
        send("x2", 1, c)
        xmerge[c, 1] = before[HALF_T:]

    def x_merge(c):
        for way in range(2):
            arrive("x1", way, c)
            xs3[c, way] = (xmerge[c, way] + xr1[c, way].astype(F32)).astype(BF16)
            send("x3", way, c)

    def finish_chunk(c):
        for way in range(2):
            arrive("x2", way, c)
        for way in range(2):
            arrive("x3", way, c)
        own = cown[c, 0] + crecv[c, 0].astype(F32)
        columns = pl.ds(c * CW, CW)
        out[pl.ds(0, HALF_T), columns] = (
            own[:HALF_T] + xr3[c, 0].astype(F32) + xr2[c, 1].astype(F32)
        ).astype(BF16)
        out[pl.ds(HALF_T, HALF_T), columns] = (
            own[HALF_T:] + xr2[c, 0].astype(F32) + xr3[c, 1].astype(F32)
        ).astype(BF16)

    local[0].wait()
    local[1].wait()
    for way in range(2):
        send("xi", way)
        send("xt", way)
    send("ci", 0)
    send("ct", 0)
    local[2].wait()
    for way in range(2):
        send("zw", way, 1, 0)
    local[3].wait()
    for way in range(2):
        send("zw", way, 1, 1)

    take_block(0)
    arrive("ci", 0)
    arrive("ct", 0)
    take_block(1)
    for k in (4, 5, 6):
        local[k].wait()
    shared_pair(0)
    local[7].wait()

    for way in range(2):
        rx = near[way]
        arrive("xi", way)
        if way == 0:
            send("xif")
        send("ci", rx)
        arrive("xt", way)
        send("xf", way)
        send("ct", rx)
    forward_rows(0)
    take_block(2)
    forward_weights(1, 0)
    take_block(6)
    forward_rows(1)
    for rx in (1, 3):
        arrive("ci", rx)
        arrive("ct", rx)
        take_block(rx * 2 + 1)
    forward_weights(1, 1)
    arrive("xif")
    send("ci", 2)
    arrive("xf", 0)
    arrive("xf", 1)
    send("ct", 2)
    take_block(4)
    forward_rows(2)
    arrive("ci", 2)
    arrive("ct", 2)
    take_block(5)
    forward_rows(6)
    shared_pair(1)
    forward_weights(2, 0)
    forward_rows(3)
    forward_rows(7)
    shared_pair(3)
    forward_weights(2, 1)
    forward_rows(4)
    down_round(0)
    forward_rows(5)
    shared_pair(2)
    for b in range(BLOCKS):
        for way in range(2):
            arrive("yr", way, b)
        arrive("yf", b)
    gate_up(0)
    forward_weights(3, 0)
    gate_up(1)
    gate_up(7)
    gate_up(2)
    gate_up(6)
    forward_weights(3, 1)
    down_round(1)
    gate_up(3)
    gate_up(5)
    down_round(2)
    forward_weights(4, 0)
    forward_weights(4, 1)
    down_round(3)
    gate_up(4)

    for c in range(NC):
        out_chunk(c)
        if c + 4 < NC + 3:
            down_round(c + 4)
        y_merge(c)
        if c > 0:
            combine(c - 1)
            core_merge(c - 1)
        if c > 1:
            x_merge(c - 2)
            finish_chunk(c - 2)
    x_merge(NC - 2)
    combine(NC - 1)
    core_merge(NC - 1)
    finish_chunk(NC - 2)
    x_merge(NC - 1)
    finish_chunk(NC - 1)
    links.finish()


def body(
    tokens,
    norm_gain,
    router_weight,
    shared_gate_vector,
    expert_ids,
    gate_weight,
    up_weight,
    down_weight,
    shared_gate_weight,
    shared_up_weight,
    shared_down_weight,
):
    ids = jnp.pad(expert_ids.T.astype(F32), ((0, 6), (0, 0)))
    anywhere = pl.BlockSpec(memory_space=pl.ANY)
    inside = pl.BlockSpec(memory_space=pltpu.VMEM)
    vmem = pltpu.VMEM
    return pl.pallas_call(
        layer_kernel,
        out_shape=jax.ShapeDtypeStruct((TOK, D), BF16),
        in_specs=[anywhere, anywhere, inside, inside, inside] + [anywhere] * 6,
        out_specs=inside,
        scratch_shapes=[
            vmem((XN, CN, TOK, D), BF16),
            vmem((XN, CN, 8, TOK), F32),
            vmem((BLOCKS * TOK, D), BF16),
            vmem((BLOCKS, TOK, TOK), BF16),
            vmem((BLOCKS, TOK, 1), F32),
            vmem((BLOCKS, TOK, 1), F32),
            vmem((YN, ROWS, D), BF16),
            vmem((ZN, D, 2 * HID), BF16),
            vmem((D, ZN * HID), BF16),
            vmem((YN, ROWS, ZN * HID), BF16),
            vmem((D, SHID), BF16),
            vmem((D, SHID), BF16),
            vmem((SHID, D), BF16),
            vmem((BLOCKS, TOK, D), F32),
            vmem((NC, ROWS, CW), F32),
            vmem((NC, 2, HALF_R, CW), F32),
        ]
        + [vmem((NC, 2, HALF_R, CW), BF16)] * 6
        + [vmem((NC, XN, TOK, CW), F32)]
        + [vmem((NC, XN, TOK, CW), BF16)] * 2
        + [vmem((NC, 2, HALF_T, CW), F32)]
        + [vmem((NC, 2, HALF_T, CW), BF16)] * 6
        + [
            pltpu.SemaphoreType.DMA((8,)),
            pltpu.SemaphoreType.DMA((COPIES,)),
            pltpu.SemaphoreType.DMA((COPIES,)),
        ],
        compiler_params=pltpu.CompilerParams(
            collective_id=0, has_side_effects=True, vmem_limit_bytes=60 * 1024 * 1024
        ),
        name="moe_layer",
    )(
        tokens,
        ids,
        norm_gain.reshape(1, D),
        router_weight,
        shared_gate_vector.reshape(1, D),
        gate_weight.reshape(D, HID),
        up_weight.reshape(D, HID),
        down_weight.reshape(D, HID),
        shared_gate_weight,
        shared_up_weight,
        shared_down_weight,
    )


def solution(mesh):
    return jax.shard_map(
        body,
        mesh=mesh,
        in_specs=(
            P(("expert", "dp"), None),
            P(),
            P(),
            P(),
            P(("expert", "dp"), None),
            P("expert", None, "dp"),
            P("expert", None, "dp"),
            P("expert", None, "dp"),
            P(None, "expert"),
            P(None, "expert"),
            P("expert", None),
        ),
        out_specs=P(("expert", "dp"), None),
        check_vma=False,
    )
```

time: 265 us -> 120 us (0.45); the launches traced: 262 us -> 120 us
  waiting for transfers between devices: 172 us -> 0 us
  Pallas kernels: 0 us -> 116 us
  matrix products: 36.4 us -> 0 us
  starting transfers between devices: 24.5 us -> 0 us
  between operations: 13.5 us -> 0.01 us
  other arithmetic: 9.47 us -> 0.69 us
  local copies, waits for them, and re-layouts: 6.03 us -> 3.12 us
    all_gather x1 -> x0, waiting for transfers between devices: 143 us -> none  [sent_together(): lax.all_gather(both, axis, axis=dim, tiled=True)]
    pallas_call x0 -> x1, Pallas kernels: none -> 116 us  [body(): pl.pallas_call(layer_kernel, out_shape=jax.ShapeDtypeStruct((TOK, D), BF1...]
    dot_general x6 -> x0, matrix products: 36.4 us -> none  [the longest x1 15.6 us: down_product(): lax.dot_general(hidden, down_piece, (((1,), (1,)), ((), ())), preferred_e...]
    all_to_all x4 -> x0, waiting for transfers between devices: 29 us -> none  [the longest x1 21 us: from_everyone(): lax.all_to_all(jnp.broadcast_to(array[None], (size, *array.shape)), axis,...]
    all_to_all x4 -> x0, starting transfers between devices: 24.5 us -> none  [the longest x1 7.26 us: body(): lax.all_to_all(outgoing, 'expert', split_axis=0, concat_axis=0, tiled=True)]
    reduce_sum x6 -> x0, other arithmetic: 5.78 us -> none  [the longest x1 2 us: summed_on_arrival(): return jnp.sum(pieces.astype(jnp.float32), axis=0)]
  transfers between devices with their start and end apart: 5 -> 0, of which waited for: 4 -> 0; matrix products, arithmetic and copies ran while one was open for 17% -> 0% of each run, Pallas kernels for 0% -> 0%
where the time goes in v1:
time: 120 us
  Pallas kernels  116 us (97%)
  local copies, waits for them, and re-layouts  3.12 us (3%)
    pallas_call x1, Pallas kernels, body(): pl.pallas_call(layer_kernel, out_shape=jax.ShapeDtypeStruct((TOK, D), BF1...  116 us
    unnamed x4, local copies, waits for them, and re-layouts  2.51 us

profile of v1, /device:TPU:4, one launch (start us, length us, event | category | flops | bytes accessed | tf_op | source)
XLA Modules:
  0.0 119.7 jit_solution(5017661220693402004)
XLA Ops:
  0.0 0.0 copy-start
  0.0 0.7 convert_bitcast_fusion
  0.7 0.6 pad.4.ids
  1.3 0.0 copy-done
  1.3 0.8 copy.12.router
  2.1 115.9 %moe_layer.1 = bf16[128,1024]{1,0:T(8,128)(2,1)} custom-call(bf16[128,1024]{1,0:T(8,128)(2,1)} %tokens.1, f32[8,128]{1,0:T(8,128)} %pad.4.ids, f32[1,1024]{1,0:T(1,128)} %bitcast.10, bf16[1024,8]{1,0:T(8,128)(2,1)} %copy.12.router, f32[1,1024]{1,0:T(1,128)} %bitcast.11, bf16[1024,128]{1,0:T(8,128)(2,1)} %bitcast.7, bf16[1024,128]{1,0:T(8,128)(2,1)} %bitcast.8, ...), custom_call_target="tpu_custom_call" | custom-call | tf_op jit(solution)/shard_map/moe_layer/pallas_call | solution.py:449
  118.0 1.7 %copy.14 = bf16[128,1024]{1,0:T(8,128)(2,1)} copy(bf16[128,1024]{1,0:T(8,128)(2,1)} %moe_layer.1) | data formatting | bytes 524288
Async XLA Ops:
  0.0 1.3 %copy-start = (bf16[1024,8]{0,1:T(8,128)(2,1)S(1)}, bf16[1024,8]{0,1:T(8,128)(2,1)}, u32[]{:S(2)}) copy-start(bf16[1024,8]{0,1:T(8,128)(2,1)} %param.13) | copy-start | bytes 49156

commit v2 on v0

v2 whole, which is shorter than its diff:
```python
import math

import jax
import jax.numpy as jnp
from jax import lax
from jax.experimental import pallas as pl
from jax.experimental.pallas import tpu as pltpu
from jax.sharding import PartitionSpec as P

MESH = pl.DeviceIdType.MESH
BF16 = jnp.bfloat16
F32 = jnp.float32

XN, CN, YN, ZN = 4, 2, 4, 8
TOK = 128
D = 1024
HID = 128
SHID = 512
CAP = 48
BLOCKS = XN * CN
ROWS = BLOCKS * CAP
WIDTHS = (128, 256, 256, 256, 128)
NC = len(WIDTHS)
COLUMNS = tuple(pl.ds(sum(WIDTHS[:c]), WIDTHS[c]) for c in range(NC))
OPP, MATE, SWAP, OWN = range(YN)
HALF_R = ROWS // 2
HALF_T = TOK // 2
COPIES = 256
OPENED_N = ("zn_{0}_1_0", "zn_{0}_3_{0}", "zn_own_1", "zn_{0}_2_0", "d_{0}_2_2")
OPENED_F = ("zf_own_1", "zf_{0}_1_0", "zf_{0}_3_{0}", "zf_own_1", "zf_{0}_3_{0}")

NT = (((1,), (1,)), ((), ()))


def dot(a, b):
    return jnp.dot(a, b, preferred_element_type=F32)


class Links:
    def __init__(self, send_sem, recv_sem):
        self.send_sem, self.recv_sem = send_sem, recv_sem
        self.copies, self.started, self.arrived, self.sizes = {}, set(), set(), {}

    def add(self, name, link, src, dst, device):
        k = len(self.copies)
        size = math.prod(src.shape) * src.dtype.itemsize
        self.sizes[name] = (link, size)
        self.copies[name] = pltpu.make_async_remote_copy(
            src_ref=src,
            dst_ref=dst,
            send_sem=self.send_sem.at[k],
            recv_sem=self.recv_sem.at[k],
            device_id=device,
            device_id_type=MESH,
        )

    def send(self, name, kind=None):
        assert (name, kind) not in self.started
        self.started.add((name, kind))
        self.copies[name].start()

    def arrive(self, name, kind=None):
        if (name, kind) not in self.arrived and (name, None) not in self.arrived:
            self.arrived.add((name, kind))
            with jax.named_scope("w_" + "_".join(map(str, name))):
                self.copies[name].wait_recv()


RATE = {"c": 600e3, "x": 46e3, "y": 46e3, "z": 92e3, "w": 92e3}
DELAY = {"c": 1.6, "x": 2.7, "y": 2.7, "z": 2.7, "w": 3.6}
LATE = {"ct": 3.0, "rm": 2.0, "rs": 2.0, "rf": 2.0, "rc": 2.0}


class Plan:
    def __init__(self, sizes):
        self.sizes = sizes
        self.tasks = {}

    def task(self, name, run, us, rank, needs=(), after=(), sends=(), kind=None):
        assert name not in self.tasks
        self.tasks[name] = (run, us, rank, tuple(needs), tuple(after), tuple(sends), kind)

    def order(self):
        now, done, arrival, lines = 0.0, set(), {}, {}
        left, steps = dict(self.tasks), []

        def kinds(copy, kind):
            along_z = self.sizes[copy][0][0] == "z"
            return (kind or "nf") if along_z else "-"

        def advance(until):
            nonlocal now
            while now < until:
                for link, lanes in lines.items():
                    busy = [q for q in lanes.values() if q]
                    for q in busy:
                        q[0][2] = RATE[link[0]] / len(busy)
                first = [q[0][1] / q[0][2] for lanes in lines.values() for q in lanes.values() if q]
                by = min([until - now] + first)
                now += by
                for link, lanes in lines.items():
                    for k, q in lanes.items():
                        if q:
                            q[0][1] -= by * q[0][2]
                            if q[0][1] < 1e-3:
                                arrival[q.pop(0)[0], k] = now + DELAY[link[0]]

        def next_event():
            soon = [t + late for (n, _), t in arrival.items() for late in (0.0, LATE.get(n[0], 0.0)) if t + late > now]
            for link, lanes in lines.items():
                busy = [q for q in lanes.values() if q]
                soon += [now + q[0][1] / (RATE[link[0]] / len(busy)) for q in busy]
            return min(soon)

        while left:
            ready = []
            for k, (name, (_, _, rank, needs, after, _, kind)) in enumerate(left.items()):
                if all(t in done for t in after) and all(
                    arrival.get((n, w), 1e9) + LATE.get(n[0], 0.0) <= now + 1e-6
                    for n in needs
                    for w in kinds(n, kind)
                ):
                    ready.append((rank, k, name))
            if not ready:
                advance(next_event())
                continue
            name = min(ready)[2]
            _, us, _, _, _, sends, kind = left.pop(name)
            steps.append((now, name))
            advance(now + us)
            done.add(name)
            for n in sends:
                link, size = self.sizes[n]
                for w in kinds(n, kind):
                    lines.setdefault(link, {}).setdefault(w, []).append([n, float(size), 1.0])
        self.end = now
        return steps


def silu_mul(g, u):
    return (g * jax.nn.sigmoid(g) * u).astype(BF16)


def layer_kernel(
    tokens, ids, gain, router, gate_vector, gate, up, down, sgate, sup, sdown, out,
    tok, idt, xn, sel, wcol, gcol, rows, frow, gu, dn, hid, sgw, suw, sdw,
    sown, ssend, srecv, pown, psend, precv, rrow, y1s, y2s, y3s, y1r, y2r, y3r,
    cown, xmerge, xs1, xs2, xs3, xr1, xr2, xr3,
    local_sem, send_sem, recv_sem,
):
    e, d = lax.axis_index("expert"), lax.axis_index("dp")
    x, core = lax.div(e, CN), lax.rem(e, CN)
    y, z = lax.div(d, ZN), lax.rem(d, ZN)
    role, odd = lax.div(y, 2), lax.rem(y, 2)
    mate_y = y + 1 - 2 * odd
    swap_y = lax.rem(y + 3 + 2 * odd, YN)
    native, foreign = core == role, core != role

    def step_x(by):
        return (lax.rem(x + by, XN) * CN + core, d)

    def step_z(by):
        return (e, y * ZN + lax.rem(z + by, ZN))

    to_x = (step_x(1), step_x(XN - 1))
    to_z = (step_z(1), step_z(ZN - 1))
    mate, swap = (e, mate_y * ZN + z), (e, swap_y * ZN + z)
    partner = (x * CN + (1 - core), d)
    cross = (x * CN + (1 - core), swap_y * ZN + z)

    first_lanes = pl.ds(0, HID)
    own_weights = (
        (gate, gu.at[0, :, first_lanes]),
        (up, gu.at[0, :, pl.ds(HID, HID)]),
        (down, dn.at[:, first_lanes]),
    )
    pairs = ((tokens, tok.at[0, 0]), (ids, idt.at[0]), *own_weights, (sgate, sgw), (sup, suw), (sdown, sdw))
    local = [pltpu.make_async_copy(src, dst, local_sem.at[i]) for i, (src, dst) in enumerate(pairs)]
    for i in (0, 1):
        local[i].start()

    @pl.when(native)
    def _():
        for i in (2, 3, 4):
            local[i].start()

    for i in (5, 6, 7):
        local[i].start()

    barrier = pltpu.get_barrier_semaphore()
    for device in (*to_x, *to_z, partner, mate, swap, cross):
        pl.semaphore_signal(barrier, inc=1, device_id=device, device_id_type=MESH)
    with jax.named_scope("meet"):
        pl.semaphore_wait(barrier, 8)

    links = Links(send_sem, recv_sem)
    add = links.add

    near = (1, 3)
    lo, hi = pl.ds(0, HALF_T), pl.ds(HALF_T, HALF_T)
    for way in range(2):
        add(("xt", way), f"x{way}", tok.at[0, 0], tok.at[near[way], 0], to_x[way])
        add(("xi", way), f"x{way}", idt.at[0], idt.at[near[way]], to_x[way])
        part = (lo, hi)[way]
        add(("xf", way), f"x{way}", tok.at[near[way], 0, part], tok.at[2, 0, part], to_x[way])
    add(("xif",), "x0", idt.at[1], idt.at[2], to_x[0])
    for rx in range(XN):
        add(("ct", rx), "c", tok.at[rx, 0], tok.at[rx, 1], partner)

    for rx in range(XN):
        span = pl.ds(rx * CAP, CAP)
        add(("rs", rx), "ys", frow.at[span], rows.at[SWAP, 0, span], swap)
        add(("rm", rx), "ym", rows.at[OWN, 0, span], rows.at[MATE, 0, span], mate)
        add(("rf", rx), "ym", rows.at[SWAP, 0, span], rows.at[OPP, 0, span], mate)
        for pos in range(YN):
            add(("rc", pos, rx), "c", rows.at[pos, 0, span], rows.at[pos, 1, span], partner)

    for k, (src, dst) in enumerate(own_weights):
        add(("w", k), "w", src, dst, cross)

    def z_slot(way, hop):
        return hop if way == 0 else (ZN - hop) % ZN

    lanes = (first_lanes, pl.ds(HID, HID))
    for hop in range(1, 5):
        for way in range(2):
            src, dst = z_slot(way, hop - 1), z_slot(way, hop)
            for which in range(2):
                if hop < 4 or which == way:
                    add(("zw", way, hop, which), f"z{way}", gu.at[src, :, lanes[which]], gu.at[dst, :, lanes[which]], to_z[way])
            for c in range(NC):
                if hop < 4 or c % 2 == way:
                    span = COLUMNS[c]
                    add(
                        ("zd", way, hop, c),
                        f"z{way}",
                        dn.at[span, pl.ds(src * HID, HID)],
                        dn.at[span, pl.ds(dst * HID, HID)],
                        to_z[way],
                    )

    for rx in range(XN):
        add(("sc", rx), "c", ssend.at[rx], srecv.at[rx], partner)
    for c in range(NC):
        cols = COLUMNS[c]
        add(("pf", c), "c", psend.at[OPP, :, cols], precv.at[OPP, :, cols], partner)
        rest = pl.ds(MATE, 3)
        add(("pn", c), "c", psend.at[rest, :, cols], precv.at[rest, :, cols], partner)
        add(("y1", c), "ym", y1s.at[:, cols], y1r.at[:, cols], mate)
        add(("y2", c), "ym", y2s.at[:, cols], y2r.at[:, cols], mate)
        add(("y3", c), "ys", y3s.at[:, cols], y3r.at[:, cols], swap)
        for way in range(2):
            add(("x1", way, c), f"x{way}", xs1.at[way, :, cols], xr1.at[way, :, cols], to_x[way])
            add(("x2", way, c), f"x{way}", xs2.at[way, :, cols], xr2.at[way, :, cols], to_x[way])
            add(("x3", way, c), f"x{way}", xs3.at[way, :, cols], xr3.at[way, :, cols], to_x[way])
    assert len(links.copies) <= COPIES

    row_iota = lax.broadcasted_iota(jnp.int32, (TOK, TOK), 0)
    lane_iota = lax.broadcasted_iota(jnp.int32, (TOK, TOK), 1)
    eye = jnp.where(row_iota == lane_iota, 1.0, 0.0).astype(BF16)
    earlier = jnp.where(lane_iota < row_iota, 1.0, 0.0).astype(BF16)
    lane = lane_iota.astype(F32)
    lane8 = lax.broadcasted_iota(jnp.int32, (TOK, BLOCKS), 1).astype(F32)
    experts = ((x * CN + role).astype(F32), (x * CN + 1 - role).astype(F32))
    plan = Plan(links.sizes)

    def step(us, rank, name, needs=(), after=(), sends=(), kind=None):
        def keep(run):
            plan.task(name, run, us, rank, needs, after, sends, kind)

        return keep

    def passing(rank, name, needs, sends, after=(), kind=None):
        plan.task(name, lambda: None, 0.03, rank, needs, after, sends, kind)

    @step(0.05, 0, "swap_weights", sends=[("w", k) for k in range(3)], kind="f")
    def _():
        pass

    @step(0.05, 0, "own_tokens", sends=[("xi", 0), ("xt", 0), ("xi", 1), ("xt", 1), ("ct", 0)])
    def _():
        local[0].wait()
        local[1].wait()

    for which in range(2):
        both_ways = [("zw", way, 1, which) for way in range(2)]

        @step(0.05, 1, f"zn_own_{which}", sends=both_ways, kind="n")
        def _(which=which):
            local[2 + which].wait()

        passing(0, f"zf_own_{which}", [("w", which)], both_ways, kind="f")

    @step(0.05, 3, "own_down_n", kind="n")
    def _():
        local[4].wait()

    passing(3, "own_down_f", [("w", 2)], [], kind="f")

    @step(0.05, 40, "own_shared")
    def _():
        for i in (5, 6, 7):
            local[i].wait()

    passing(1, "x_ids", [("xi", 0)], [("xif",)])
    for way in range(2):
        passing(2, f"x_tok_{way}", [("xt", way)], [("xf", way), ("ct", near[way])])
    passing(2, "x_far", [("xf", 0), ("xf", 1)], [("ct", 2)])

    def normed(rx, cc):
        wide = tok[rx, cc].astype(F32)
        mean_square = jnp.mean(wide * wide, axis=-1, keepdims=True)
        n = (wide * lax.rsqrt(mean_square + 1e-06) * gain[...]).astype(BF16)
        b = 2 * rx + cc
        xn[pl.ds(b * TOK, TOK), :] = n
        gcol[b] = jax.nn.sigmoid(
            jnp.sum(n.astype(F32) * gate_vector[...], axis=-1, keepdims=True)
        )
        return n

    def take_block(rx):
        needs = ([], [], [("xif",)], [("xi", 1)])[rx]
        after = ["own_tokens"] if rx == 0 else ["x_ids", ("", "x_tok_0", "x_far", "x_tok_1")[rx]]

        @step(1.1, 20, f"take_{rx}", needs, after, [("rs", rx), ("rm", rx), ("rc", OWN, rx)])
        def _():
            n = normed(rx, 0)
            logits = lax.dot_general(n, router[...], NT, preferred_element_type=F32)
            columns = lax.dot_general(
                eye, idt[rx].astype(F32).astype(BF16), NT, preferred_element_type=F32
            )
            id0, id1 = columns[:, 0:1], columns[:, 1:2]
            l0 = jnp.sum(jnp.where(lane8 == id0, logits, 0.0), axis=-1, keepdims=True)
            l1 = jnp.sum(jnp.where(lane8 == id1, logits, 0.0), axis=-1, keepdims=True)
            w0 = jax.nn.sigmoid(l0 - l1)
            span = pl.ds(rx * CAP, CAP)
            for k in (1, 0):
                is0, is1 = id0 == experts[k], id1 == experts[k]
                wcol[k, rx] = jnp.where(is0, w0, 0.0) + jnp.where(is1, 1.0 - w0, 0.0)
                named = jnp.where(is0, 1.0, 0.0) + jnp.where(is1, 1.0, 0.0)
                named = jnp.broadcast_to(named, (TOK, TOK))
                slot = dot(earlier, named.astype(BF16))
                chosen = jnp.where(slot == lane, named, 0.0)
                sel[k, rx] = chosen.astype(BF16)
                table = jnp.transpose(chosen)[0:CAP, :].astype(BF16)
                found = dot(table, n).astype(BF16)
                if k == 0:
                    rows[OWN, 0, span, :] = found
                else:
                    frow[span, :] = found

    def take_other(rx):
        @step(0.35, 35, f"other_{rx}", [("ct", rx)])
        def _():
            normed(rx, 1)

    def shared_pair(rx):
        @step(1.07, 50, f"shared_{rx}", [], ["own_shared", f"take_{rx}", f"other_{rx}"], [("sc", rx)])
        def _():
            a = xn[pl.ds(rx * 2 * TOK, 2 * TOK), :]
            hidden = silu_mul(dot(a, sgw[...]), dot(a, suw[...]))
            part = dot(hidden, sdw[...])
            sown[rx] = part[:TOK] * gcol[2 * rx]
            ssend[rx] = (part[TOK:] * gcol[2 * rx + 1]).astype(BF16)

    every_row = []
    for rx in range(XN):
        take_block(rx)
        take_other(rx)
        shared_pair(rx)
        passing(4, f"rows_mate_{rx}", [("rm", rx)], [("rc", MATE, rx)])
        passing(4, f"rows_swap_{rx}", [("rs", rx)], [("rf", rx), ("rc", SWAP, rx)])
        passing(4, f"rows_opp_{rx}", [("rf", rx)], [("rc", OPP, rx)])
        every_row += [("rc", pos, rx) for pos in range(YN)]
    rows_here = [f"rows_{k}_{rx}" for k in ("mate", "swap", "opp") for rx in range(XN)]

    of_slot = {s: [] for s in range(ZN)}
    for kind in "nf":
        of_slot[0] += [f"z{kind}_own_{which}" for which in range(2)]
        for hop in range(1, 5):
            for which in range(2):
                for way in range(2):
                    if ("zw", way, hop, which) in links.copies:
                        onward = [("zw", way, hop + 1, which)]
                        onward = [n for n in onward if n in links.copies]
                        name = f"z{kind}_{way}_{hop}_{which}"
                        passing(0, name, [("zw", way, hop, which)], onward, kind=kind)
                        of_slot[z_slot(way, hop)].append(name)
    for c in range(NC):
        for way in range(2):
            for kind, opened in (("n", OPENED_N), ("f", OPENED_F)):
                last = [f"own_down_{kind}", opened[c].format(way)]
                passing(1, f"d{kind}_{way}_1_{c}", [], [("zd", way, 1, c)], last, kind)
            for hop in range(2, 5):
                if ("zd", way, hop, c) in links.copies:
                    passing(1, f"d_{way}_{hop}_{c}", [("zd", way, hop - 1, c)], [("zd", way, hop, c)])

    def gate_up(s):
        @step(1.0, 30, f"gate_up_{s}", every_row, of_slot[s] + rows_here)
        def _():
            for k in range(YN):
                both = dot(rows[k].reshape(ROWS, D), gu[s])
                hid[pl.ds(k * ROWS, ROWS), pl.ds(s * HID, HID)] = silu_mul(both[:, :HID], both[:, HID:])

    for s in (0, 1, 7, 2, 6, 3, 5, 4):
        gate_up(s)
    hidden_done = [f"gate_up_{s}" for s in range(ZN)]

    def way_back(c):
        columns = COLUMNS[c]
        needs = [n for n in links.copies if n[0] == "zd" and n[3] == c]

        def down_out(first, many):
            h = hid[pl.ds(first * ROWS, many * ROWS), :]
            part = lax.dot_general(h, dn[columns, :], NT, preferred_element_type=F32)
            for k in range(many):
                pown[first + k, :, columns] = part[k * ROWS : k * ROWS + HALF_R]
                psend[first + k, :, columns] = part[k * ROWS + HALF_R : (k + 1) * ROWS].astype(BF16)

        def chip(pos):
            return pown[pos, :, columns] + precv[pos, :, columns].astype(F32)

        @step(0.6, 25, f"far_{c}", needs, hidden_done + ["own_down_n", "own_down_f"], [("pf", c)])
        def _():
            down_out(OPP, 1)

        @step(1.4, 25, f"near_{c}", [], [f"far_{c}"], [("pn", c)])
        def _():
            down_out(MATE, 3)

        @step(0.1, 9, f"opp_{c}", [("pf", c)], [f"near_{c}"], [("y1", c)])
        def _():
            y1s[:, columns] = chip(OPP).astype(BF16)

        @step(0.1, 9, f"mate_{c}", [("pn", c)], [f"near_{c}"], [("y2", c)])
        def _():
            y2s[:, columns] = chip(MATE).astype(BF16)

        @step(0.1, 8, f"swap_{c}", [("y1", c), ("pn", c)], [f"near_{c}"], [("y3", c)])
        def _():
            y3s[:, columns] = (chip(SWAP) + y1r[:, columns].astype(F32)).astype(BF16)

        @step(
            0.45, 8, f"combine_{c}",
            [("y2", c), ("y3", c), ("pn", c)] + [("sc", rx) for rx in range(XN)],
            [f"near_{c}"] + [f"shared_{rx}" for rx in range(XN)],
            [("x1", 0, c), ("x1", 1, c), ("x2", 0, c), ("x2", 1, c)],
        )
        def _():
            rrow[:, columns] = (chip(OWN) + y2r[:, columns].astype(F32)).astype(BF16)

            def part(rx):
                span = pl.ds(rx * CAP, CAP)
                here = dot(sel[0, rx][:, :CAP], rrow[span, columns]) * wcol[0, rx]
                there = dot(sel[1, rx][:, :CAP], y3r[span, columns]) * wcol[1, rx]
                return here + there + sown[rx, :, columns] + srecv[rx, :, columns].astype(F32)

            far = part(2)
            xs1[0, :, columns] = far[:HALF_T].astype(BF16)
            xs1[1, :, columns] = far[HALF_T:].astype(BF16)
            after = part(3)
            xs2[0, :, columns] = after[HALF_T:].astype(BF16)
            xmerge[0, :, columns] = after[:HALF_T]
            before = part(1)
            xs2[1, :, columns] = before[:HALF_T].astype(BF16)
            xmerge[1, :, columns] = before[HALF_T:]
            cown[:, columns] = part(0)

        def x_merge(way):
            @step(0.06, 7, f"x_merge_{way}_{c}", [("x1", way, c)], [f"combine_{c}"], [("x3", way, c)])
            def _():
                xs3[way, :, columns] = (
                    xmerge[way, :, columns] + xr1[way, :, columns].astype(F32)
                ).astype(BF16)

        x_merge(0)
        x_merge(1)

        @step(0.1, 12, f"finish_{c}", [(k, way, c) for k in ("x2", "x3") for way in range(2)], [f"combine_{c}"])
        def _():
            own = cown[:, columns]
            out[pl.ds(0, HALF_T), columns] = (
                own[:HALF_T] + xr3[0, :, columns].astype(F32) + xr2[1, :, columns].astype(F32)
            ).astype(BF16)
            out[pl.ds(HALF_T, HALF_T), columns] = (
                own[HALF_T:] + xr2[0, :, columns].astype(F32) + xr3[1, :, columns].astype(F32)
            ).astype(BF16)

    for c in range(NC):
        way_back(c)

    only = {"n": native, "f": foreign}
    for _, name in plan.order():
        run, _, _, needs, _, sends, kind = plan.tasks[name]

        def carry_out(run=run, needs=needs, sends=sends, name=name, kind=kind):
            for n in needs:
                links.arrive(n, kind)
            with jax.named_scope(name):
                run()
            for n in sends:
                links.send(n, kind)

        if kind is None:
            carry_out()
        else:
            pl.when(only[kind])(carry_out)
    for name in links.copies:
        whole = ({None}, {"f"} if name[0] == "w" else {"n", "f"})
        assert {k for m, k in links.started if m == name} in whole
        assert {k for m, k in links.arrived if m == name} in whole
    with jax.named_scope("finish"):

        @pl.when(foreign)
        def _():
            for k in range(3):
                links.copies["w", k].wait_send()

        for name, copy in links.copies.items():
            if name[0] != "w":
                copy.wait_send()


def body(
    tokens,
    norm_gain,
    router_weight,
    shared_gate_vector,
    expert_ids,
    gate_weight,
    up_weight,
    down_weight,
    shared_gate_weight,
    shared_up_weight,
    shared_down_weight,
):
    anywhere = pl.BlockSpec(memory_space=pl.ANY)
    inside = pl.BlockSpec(memory_space=pltpu.VMEM)
    vmem = pltpu.VMEM
    return pl.pallas_call(
        layer_kernel,
        out_shape=jax.ShapeDtypeStruct((TOK, D), BF16),
        in_specs=[anywhere, anywhere, inside, inside, inside] + [anywhere] * 6,
        out_specs=inside,
        scratch_shapes=[
            vmem((XN, CN, TOK, D), BF16),
            vmem((XN, 2, TOK), jnp.int32),
            vmem((BLOCKS * TOK, D), BF16),
            vmem((2, XN, TOK, TOK), BF16),
            vmem((2, XN, TOK, 1), F32),
            vmem((BLOCKS, TOK, 1), F32),
            vmem((YN, 2, HALF_R, D), BF16),
            vmem((HALF_R, D), BF16),
            vmem((ZN, D, 2 * HID), BF16),
            vmem((D, ZN * HID), BF16),
            vmem((YN * ROWS, ZN * HID), BF16),
            vmem((D, SHID), BF16),
            vmem((D, SHID), BF16),
            vmem((SHID, D), BF16),
            vmem((XN, TOK, D), F32),
            vmem((XN, TOK, D), BF16),
            vmem((XN, TOK, D), BF16),
            vmem((YN, HALF_R, D), F32),
            vmem((YN, HALF_R, D), BF16),
            vmem((YN, HALF_R, D), BF16),
        ]
        + [vmem((HALF_R, D), BF16)] * 7
        + [vmem((TOK, D), F32), vmem((2, HALF_T, D), F32)]
        + [vmem((2, HALF_T, D), BF16)] * 6
        + [
            pltpu.SemaphoreType.DMA((8,)),
            pltpu.SemaphoreType.DMA((COPIES,)),
            pltpu.SemaphoreType.DMA((COPIES,)),
        ],
        compiler_params=pltpu.CompilerParams(
            collective_id=0, has_side_effects=True, vmem_limit_bytes=60 * 1024 * 1024
        ),
        name="moe_layer",
    )(
        tokens,
        expert_ids.T,
        norm_gain.reshape(1, D),
        router_weight.T,
        shared_gate_vector.reshape(1, D),
        gate_weight.reshape(D, HID),
        up_weight.reshape(D, HID),
        down_weight.reshape(D, HID),
        shared_gate_weight,
        shared_up_weight,
        shared_down_weight,
    )


def solution(mesh):
    return jax.shard_map(
        body,
        mesh=mesh,
        in_specs=(
            P(("expert", "dp"), None),
            P(),
            P(),
            P(),
            P(("expert", "dp"), None),
            P("expert", None, "dp"),
            P("expert", None, "dp"),
            P("expert", None, "dp"),
            P(None, "expert"),
            P(None, "expert"),
            P("expert", None),
        ),
        out_specs=P(("expert", "dp"), None),
        check_vma=False,
    )
```

time: 265 us -> 102 us (0.38); the launches traced: 262 us -> 102 us
  waiting for transfers between devices: 172 us -> 0 us
  Pallas kernels: 0 us -> 100 us
  matrix products: 36.4 us -> 0 us
  starting transfers between devices: 24.5 us -> 0 us
  between operations: 13.5 us -> 0.01 us
  other arithmetic: 9.47 us -> 0 us
  local copies, waits for them, and re-layouts: 6.03 us -> 1.67 us
    all_gather x1 -> x0, waiting for transfers between devices: 143 us -> none  [sent_together(): lax.all_gather(both, axis, axis=dim, tiled=True)]
    pallas_call x0 -> x1, Pallas kernels: none -> 100 us  [body(): pl.pallas_call(layer_kernel, out_shape=jax.ShapeDtypeStruct((TOK, D), BF1...]
    dot_general x6 -> x0, matrix products: 36.4 us -> none  [the longest x1 15.6 us: down_product(): lax.dot_general(hidden, down_piece, (((1,), (1,)), ((), ())), preferred_e...]
    all_to_all x4 -> x0, waiting for transfers between devices: 29 us -> none  [the longest x1 21 us: from_everyone(): lax.all_to_all(jnp.broadcast_to(array[None], (size, *array.shape)), axis,...]
    all_to_all x4 -> x0, starting transfers between devices: 24.5 us -> none  [the longest x1 7.26 us: body(): lax.all_to_all(outgoing, 'expert', split_axis=0, concat_axis=0, tiled=True)]
    reduce_sum x6 -> x0, other arithmetic: 5.78 us -> none  [the longest x1 2 us: summed_on_arrival(): return jnp.sum(pieces.astype(jnp.float32), axis=0)]
  transfers between devices with their start and end apart: 5 -> 0, of which waited for: 4 -> 0; matrix products, arithmetic and copies ran while one was open for 17% -> 0% of each run, Pallas kernels for 0% -> 0%
where the time goes in v2:
time: 102 us
  Pallas kernels  100 us (98%)
  local copies, waits for them, and re-layouts  1.67 us (2%)
    pallas_call x1, Pallas kernels, body(): pl.pallas_call(layer_kernel, out_shape=jax.ShapeDtypeStruct((TOK, D), BF1...  100 us

profile of v2, /device:TPU:4, one launch (start us, length us, event | category | flops | bytes accessed | tf_op | source)
XLA Modules:
  0.0 101.8 jit_solution(17642262274016425523)
XLA Ops:
  0.0 100.2 %moe_layer.1 = bf16[128,1024]{1,0:T(8,128)(2,1)} custom-call(bf16[128,1024]{1,0:T(8,128)(2,1)} %tokens.1, s32[2,128]{1,0:T(2,128)} %bitcast.13, f32[1,1024]{1,0:T(1,128)} %bitcast.11, bf16[8,1024]{1,0:T(8,128)(2,1)} %bitcast.10, f32[1,1024]{1,0:T(1,128)} %bitcast.12, bf16[1024,128]{1,0:T(8,128)(2,1)} %bitcast.7, bf16[1024,128]{1,0:T(8,128)(2,1)} %bitcast.8, ...), custom_call_target="tpu_custom_call" | custom-call | tf_op jit(solution)/shard_map/moe_layer/pallas_call | solution.py:540
  100.2 1.7 %copy.13 = bf16[128,1024]{1,0:T(8,128)(2,1)} copy(bf16[128,1024]{1,0:T(8,128)(2,1)} %moe_layer.1) | data formatting | bytes 524288

commit v3 on v2

--- a/solution.py
+++ b/solution.py
@@ -1,5 +1,3 @@
-import math
-
 import jax
 import jax.numpy as jnp
 from jax import lax
@@ -19,15 +17,16 @@
 CAP = 48
 BLOCKS = XN * CN
 ROWS = BLOCKS * CAP
-WIDTHS = (128, 256, 256, 256, 128)
+WIDTHS = (256, 256, 256, 256)
 NC = len(WIDTHS)
 COLUMNS = tuple(pl.ds(sum(WIDTHS[:c]), WIDTHS[c]) for c in range(NC))
+PARTS = [(columns,) for columns in COLUMNS[:-1]]
+PARTS.append(tuple(pl.ds(D - WIDTHS[-1] + at, WIDTHS[-1] // 2) for at in (0, WIDTHS[-1] // 2)))
+OTHERS = pl.ds(WIDTHS[0], D - WIDTHS[0])
 OPP, MATE, SWAP, OWN = range(YN)
 HALF_R = ROWS // 2
 HALF_T = TOK // 2
 COPIES = 256
-OPENED_N = ("zn_{0}_1_0", "zn_{0}_3_{0}", "zn_own_1", "zn_{0}_2_0", "d_{0}_2_2")
-OPENED_F = ("zf_own_1", "zf_{0}_1_0", "zf_{0}_3_{0}", "zf_own_1", "zf_{0}_3_{0}")
 
 NT = (((1,), (1,)), ((), ()))
 
@@ -39,12 +38,10 @@
 class Links:
     def __init__(self, send_sem, recv_sem):
         self.send_sem, self.recv_sem = send_sem, recv_sem
-        self.copies, self.started, self.arrived, self.sizes = {}, set(), set(), {}
+        self.copies, self.started, self.arrived = {}, set(), set()
 
     def add(self, name, link, src, dst, device):
         k = len(self.copies)
-        size = math.prod(src.shape) * src.dtype.itemsize
-        self.sizes[name] = (link, size)
         self.copies[name] = pltpu.make_async_remote_copy(
             src_ref=src,
             dst_ref=dst,
@@ -66,14 +63,18 @@
                 self.copies[name].wait_recv()
 
 
-RATE = {"c": 600e3, "x": 46e3, "y": 46e3, "z": 92e3, "w": 92e3}
-DELAY = {"c": 1.6, "x": 2.7, "y": 2.7, "z": 2.7, "w": 3.6}
-LATE = {"ct": 3.0, "rm": 2.0, "rs": 2.0, "rf": 2.0, "rc": 2.0}
+STEPS = (
+    5, 0, 3, 2, 7, 67, 98, 4, 10, 6, 42, 8, 68, 40, 15, 12, 11, 13, 33, 41, 73, 76, 90, 1, 53, 19, 69, 55, 54, 72, 14,
+    46, 56, 16, 27, 85, 39, 9, 81, 99, 57, 18, 77, 22, 37, 21, 45, 17, 20, 44, 86, 70, 31, 58, 30, 80, 59, 25, 74, 61,
+    32, 34, 28, 38, 60, 43, 48, 82, 36, 78, 87, 24, 26, 23, 35, 75, 107, 71, 50, 91, 47, 83, 106, 105, 63, 62, 64,
+    109, 103, 94, 49, 108, 65, 100, 95, 92, 104, 88, 79, 84, 52, 51, 66, 110, 111, 96, 101, 112, 89, 93, 113, 120,
+    114, 97, 102, 121, 122, 129, 130, 131, 115, 123, 138, 139, 147, 124, 140, 29, 133, 132, 116, 148, 149, 141, 125,
+    142, 117, 118, 134, 150, 143, 119, 127, 136, 126, 135, 151, 152, 144, 145, 128, 153, 137, 146,
+)
 
 
 class Plan:
-    def __init__(self, sizes):
-        self.sizes = sizes
+    def __init__(self):
         self.tasks = {}
 
     def task(self, name, run, us, rank, needs=(), after=(), sends=(), kind=None):
@@ -81,60 +82,13 @@
         self.tasks[name] = (run, us, rank, tuple(needs), tuple(after), tuple(sends), kind)
 
     def order(self):
-        now, done, arrival, lines = 0.0, set(), {}, {}
-        left, steps = dict(self.tasks), []
-
-        def kinds(copy, kind):
-            along_z = self.sizes[copy][0][0] == "z"
-            return (kind or "nf") if along_z else "-"
-
-        def advance(until):
-            nonlocal now
-            while now < until:
-                for link, lanes in lines.items():
-                    busy = [q for q in lanes.values() if q]
-                    for q in busy:
-                        q[0][2] = RATE[link[0]] / len(busy)
-                first = [q[0][1] / q[0][2] for lanes in lines.values() for q in lanes.values() if q]
-                by = min([until - now] + first)
-                now += by
-                for link, lanes in lines.items():
-                    for k, q in lanes.items():
-                        if q:
-                            q[0][1] -= by * q[0][2]
-                            if q[0][1] < 1e-3:
-                                arrival[q.pop(0)[0], k] = now + DELAY[link[0]]
-
-        def next_event():
-            soon = [t + late for (n, _), t in arrival.items() for late in (0.0, LATE.get(n[0], 0.0)) if t + late > now]
-            for link, lanes in lines.items():
-                busy = [q for q in lanes.values() if q]
-                soon += [now + q[0][1] / (RATE[link[0]] / len(busy)) for q in busy]
-            return min(soon)
-
-        while left:
-            ready = []
-            for k, (name, (_, _, rank, needs, after, _, kind)) in enumerate(left.items()):
-                if all(t in done for t in after) and all(
-                    arrival.get((n, w), 1e9) + LATE.get(n[0], 0.0) <= now + 1e-6
-                    for n in needs
-                    for w in kinds(n, kind)
-                ):
-                    ready.append((rank, k, name))
-            if not ready:
-                advance(next_event())
-                continue
-            name = min(ready)[2]
-            _, us, _, _, _, sends, kind = left.pop(name)
-            steps.append((now, name))
-            advance(now + us)
+        names = list(self.tasks)
+        assert sorted(STEPS) == list(range(len(names)))
+        done = set()
+        for name in (names[k] for k in STEPS):
+            assert done.issuperset(self.tasks[name][4])
             done.add(name)
-            for n in sends:
-                link, size = self.sizes[n]
-                for w in kinds(n, kind):
-                    lines.setdefault(link, {}).setdefault(w, []).append([n, float(size), 1.0])
-        self.end = now
-        return steps
+            yield name
 
 
 def silu_mul(g, u):
@@ -145,7 +99,7 @@
     tokens, ids, gain, router, gate_vector, gate, up, down, sgate, sup, sdown, out,
     tok, idt, xn, sel, wcol, gcol, rows, frow, gu, dn, hid, sgw, suw, sdw,
     sown, ssend, srecv, pown, psend, precv, rrow, y1s, y2s, y3s, y1r, y2r, y3r,
-    cown, xmerge, xs1, xs2, xs3, xr1, xr2, xr3,
+    cown, xmerge, xs1, xs2, xs3, xr1, xr2, xr3, aside,
     local_sem, send_sem, recv_sem,
 ):
     e, d = lax.axis_index("expert"), lax.axis_index("dp")
@@ -172,19 +126,28 @@
     own_weights = (
         (gate, gu.at[0, :, first_lanes]),
         (up, gu.at[0, :, pl.ds(HID, HID)]),
-        (down, dn.at[:, first_lanes]),
+        (down.at[COLUMNS[0]], dn.at[COLUMNS[0], first_lanes]),
+        (down.at[OTHERS], dn.at[OTHERS, first_lanes]),
     )
     pairs = ((tokens, tok.at[0, 0]), (ids, idt.at[0]), *own_weights, (sgate, sgw), (sup, suw), (sdown, sdw))
     local = [pltpu.make_async_copy(src, dst, local_sem.at[i]) for i, (src, dst) in enumerate(pairs)]
     for i in (0, 1):
         local[i].start()
 
+    given = ((gate, aside.at[0]), (up, aside.at[1]), (down, aside.at[2]))
+    lent = [pltpu.make_async_copy(src, dst, local_sem.at[2 + i]) for i, (src, dst) in enumerate(given)]
+
     @pl.when(native)
     def _():
-        for i in (2, 3, 4):
+        for i in (2, 3, 4, 5):
             local[i].start()
 
-    for i in (5, 6, 7):
+    @pl.when(foreign)
+    def _():
+        for copy in lent:
+            copy.start()
+
+    for i in (6, 7, 8):
         local[i].start()
 
     barrier = pltpu.get_barrier_semaphore()
@@ -209,14 +172,15 @@
 
     for rx in range(XN):
         span = pl.ds(rx * CAP, CAP)
-        add(("rs", rx), "ys", frow.at[span], rows.at[SWAP, 0, span], swap)
-        add(("rm", rx), "ym", rows.at[OWN, 0, span], rows.at[MATE, 0, span], mate)
-        add(("rf", rx), "ym", rows.at[SWAP, 0, span], rows.at[OPP, 0, span], mate)
+        add(("rs", rx), "s", frow.at[span], rows.at[SWAP, 0, span], swap)
+        add(("rm", rx), "y", rows.at[OWN, 0, span], rows.at[MATE, 0, span], mate)
+        add(("rf", rx), "y", rows.at[SWAP, 0, span], rows.at[OPP, 0, span], mate)
         for pos in range(YN):
             add(("rc", pos, rx), "c", rows.at[pos, 0, span], rows.at[pos, 1, span], partner)
 
-    for k, (src, dst) in enumerate(own_weights):
-        add(("w", k), "w", src, dst, cross)
+    sources = (aside.at[0], aside.at[1], aside.at[2, COLUMNS[0]], aside.at[2, OTHERS])
+    for k, (src, (_, dst)) in enumerate(zip(sources, own_weights)):
+        add(("w", k), "s", src, dst, cross)
 
     def z_slot(way, hop):
         return hop if way == 0 else (ZN - hop) % ZN
@@ -246,13 +210,14 @@
         add(("pf", c), "c", psend.at[OPP, :, cols], precv.at[OPP, :, cols], partner)
         rest = pl.ds(MATE, 3)
         add(("pn", c), "c", psend.at[rest, :, cols], precv.at[rest, :, cols], partner)
-        add(("y1", c), "ym", y1s.at[:, cols], y1r.at[:, cols], mate)
-        add(("y2", c), "ym", y2s.at[:, cols], y2r.at[:, cols], mate)
-        add(("y3", c), "ys", y3s.at[:, cols], y3r.at[:, cols], swap)
-        for way in range(2):
-            add(("x1", way, c), f"x{way}", xs1.at[way, :, cols], xr1.at[way, :, cols], to_x[way])
-            add(("x2", way, c), f"x{way}", xs2.at[way, :, cols], xr2.at[way, :, cols], to_x[way])
-            add(("x3", way, c), f"x{way}", xs3.at[way, :, cols], xr3.at[way, :, cols], to_x[way])
+        for p, cols in enumerate(PARTS[c]):
+            add(("y1", c, p), "y", y1s.at[:, cols], y1r.at[:, cols], mate)
+            add(("y2", c, p), "y", y2s.at[:, cols], y2r.at[:, cols], mate)
+            add(("y3", c, p), "s", y3s.at[:, cols], y3r.at[:, cols], swap)
+            for way in range(2):
+                add(("x1", way, c, p), f"x{way}", xs1.at[way, :, cols], xr1.at[way, :, cols], to_x[way])
+                add(("x2", way, c, p), f"x{way}", xs2.at[way, :, cols], xr2.at[way, :, cols], to_x[way])
+                add(("x3", way, c, p), f"x{way}", xs3.at[way, :, cols], xr3.at[way, :, cols], to_x[way])
     assert len(links.copies) <= COPIES
 
     row_iota = lax.broadcasted_iota(jnp.int32, (TOK, TOK), 0)
@@ -262,7 +227,7 @@
     lane = lane_iota.astype(F32)
     lane8 = lax.broadcasted_iota(jnp.int32, (TOK, BLOCKS), 1).astype(F32)
     experts = ((x * CN + role).astype(F32), (x * CN + 1 - role).astype(F32))
-    plan = Plan(links.sizes)
+    plan = Plan()
 
     def step(us, rank, name, needs=(), after=(), sends=(), kind=None):
         def keep(run):
@@ -273,9 +238,12 @@
     def passing(rank, name, needs, sends, after=(), kind=None):
         plan.task(name, lambda: None, 0.03, rank, needs, after, sends, kind)
 
-    @step(0.05, 0, "swap_weights", sends=[("w", k) for k in range(3)], kind="f")
+    @step(0.03, 0, "swap_weights", sends=[("w", 0), ("w", 1), ("w", 2)], kind="f")
     def _():
-        pass
+        for copy in lent:
+            copy.wait()
+
+    passing(0, "swap_down", [], [("w", 3)], ["take_3"], "f")
 
     @step(0.05, 0, "own_tokens", sends=[("xi", 0), ("xt", 0), ("xi", 1), ("xt", 1), ("ct", 0)])
     def _():
@@ -294,12 +262,14 @@
     @step(0.05, 3, "own_down_n", kind="n")
     def _():
         local[4].wait()
-
-    passing(3, "own_down_f", [("w", 2)], [], kind="f")
+        local[5].wait()
+
+    passing(1, "own_down_first", [("w", 2)], [], kind="f")
+    passing(3, "own_down_f", [("w", 3)], [], ["own_down_first"], "f")
 
     @step(0.05, 40, "own_shared")
     def _():
-        for i in (5, 6, 7):
+        for i in (6, 7, 8):
             local[i].wait()
 
     passing(1, "x_ids", [("xi", 0)], [("xif",)])
@@ -388,9 +358,9 @@
                         of_slot[z_slot(way, hop)].append(name)
     for c in range(NC):
         for way in range(2):
-            for kind, opened in (("n", OPENED_N), ("f", OPENED_F)):
-                last = [f"own_down_{kind}", opened[c].format(way)]
-                passing(1, f"d{kind}_{way}_1_{c}", [], [("zd", way, 1, c)], last, kind)
+            for kind in "nf":
+                here = "own_down_first" if kind == "f" and c == 0 else f"own_down_{kind}"
+                passing(1, f"d{kind}_{way}_1_{c}", [], [("zd", way, 1, c)], [here], kind)
             for hop in range(2, 5):
                 if ("zd", way, hop, c) in links.copies:
                     passing(1, f"d_{way}_{hop}_{c}", [("zd", way, hop - 1, c)], [("zd", way, hop, c)])
@@ -417,34 +387,37 @@
                 pown[first + k, :, columns] = part[k * ROWS : k * ROWS + HALF_R]
                 psend[first + k, :, columns] = part[k * ROWS + HALF_R : (k + 1) * ROWS].astype(BF16)
 
+        @step(0.6, 24, f"far_{c}", needs, hidden_done + ["own_down_n", "own_down_f"], [("pf", c)])
+        def _():
+            down_out(OPP, 1)
+
+        @step(1.4, 25, f"near_{c}", [], [f"far_{c}"], [("pn", c)])
+        def _():
+            down_out(MATE, 3)
+
+    def home(c, p):
+        columns = PARTS[c][p]
+
         def chip(pos):
             return pown[pos, :, columns] + precv[pos, :, columns].astype(F32)
 
-        @step(0.6, 25, f"far_{c}", needs, hidden_done + ["own_down_n", "own_down_f"], [("pf", c)])
-        def _():
-            down_out(OPP, 1)
-
-        @step(1.4, 25, f"near_{c}", [], [f"far_{c}"], [("pn", c)])
-        def _():
-            down_out(MATE, 3)
-
-        @step(0.1, 9, f"opp_{c}", [("pf", c)], [f"near_{c}"], [("y1", c)])
+        @step(0.1, 9, f"opp_{c}_{p}", [("pf", c)], [f"near_{c}"], [("y1", c, p)])
         def _():
             y1s[:, columns] = chip(OPP).astype(BF16)
 
-        @step(0.1, 9, f"mate_{c}", [("pn", c)], [f"near_{c}"], [("y2", c)])
+        @step(0.1, 9, f"mate_{c}_{p}", [("pn", c)], [f"near_{c}"], [("y2", c, p)])
         def _():
             y2s[:, columns] = chip(MATE).astype(BF16)
 
-        @step(0.1, 8, f"swap_{c}", [("y1", c), ("pn", c)], [f"near_{c}"], [("y3", c)])
+        @step(0.1, 8, f"swap_{c}_{p}", [("y1", c, p), ("pn", c)], [f"near_{c}"], [("y3", c, p)])
         def _():
             y3s[:, columns] = (chip(SWAP) + y1r[:, columns].astype(F32)).astype(BF16)
 
         @step(
-            0.45, 8, f"combine_{c}",
-            [("y2", c), ("y3", c), ("pn", c)] + [("sc", rx) for rx in range(XN)],
+            0.45, 8, f"combine_{c}_{p}",
+            [("y2", c, p), ("y3", c, p), ("pn", c)] + [("sc", rx) for rx in range(XN)],
             [f"near_{c}"] + [f"shared_{rx}" for rx in range(XN)],
-            [("x1", 0, c), ("x1", 1, c), ("x2", 0, c), ("x2", 1, c)],
+            [("x1", 0, c, p), ("x1", 1, c, p), ("x2", 0, c, p), ("x2", 1, c, p)],
         )
         def _():
             rrow[:, columns] = (chip(OWN) + y2r[:, columns].astype(F32)).astype(BF16)
@@ -467,7 +440,7 @@
             cown[:, columns] = part(0)
 
         def x_merge(way):
-            @step(0.06, 7, f"x_merge_{way}_{c}", [("x1", way, c)], [f"combine_{c}"], [("x3", way, c)])
+            @step(0.06, 7, f"x_merge_{way}_{c}_{p}", [("x1", way, c, p)], [f"combine_{c}_{p}"], [("x3", way, c, p)])
             def _():
                 xs3[way, :, columns] = (
                     xmerge[way, :, columns] + xr1[way, :, columns].astype(F32)
@@ -476,7 +449,7 @@
         x_merge(0)
         x_merge(1)
 
-        @step(0.1, 12, f"finish_{c}", [(k, way, c) for k in ("x2", "x3") for way in range(2)], [f"combine_{c}"])
+        @step(0.1, 12, f"finish_{c}_{p}", [(k, way, c, p) for k in ("x2", "x3") for way in range(2)], [f"combine_{c}_{p}"])
         def _():
             own = cown[:, columns]
             out[pl.ds(0, HALF_T), columns] = (
@@ -488,9 +461,11 @@
 
     for c in range(NC):
         way_back(c)
+        for p in range(len(PARTS[c])):
+            home(c, p)
 
     only = {"n": native, "f": foreign}
-    for _, name in plan.order():
+    for name in plan.order():
         run, _, _, needs, _, sends, kind = plan.tasks[name]
 
         def carry_out(run=run, needs=needs, sends=sends, name=name, kind=kind):
@@ -513,7 +488,7 @@
 
         @pl.when(foreign)
         def _():
-            for k in range(3):
+            for k in range(len(own_weights)):
                 links.copies["w", k].wait_send()
 
         for name, copy in links.copies.items():
@@ -539,7 +514,7 @@
     vmem = pltpu.VMEM
     return pl.pallas_call(
         layer_kernel,
-        out_shape=jax.ShapeDtypeStruct((TOK, D), BF16),
+        out_shape=pltpu.VMEM((TOK, D), BF16),
         in_specs=[anywhere, anywhere, inside, inside, inside] + [anywhere] * 6,
         out_specs=inside,
         scratch_shapes=[
@@ -567,8 +542,9 @@
         + [vmem((HALF_R, D), BF16)] * 7
         + [vmem((TOK, D), F32), vmem((2, HALF_T, D), F32)]
         + [vmem((2, HALF_T, D), BF16)] * 6
+        + [vmem((3, D, HID), BF16)]
         + [
-            pltpu.SemaphoreType.DMA((8,)),
+            pltpu.SemaphoreType.DMA((9,)),
             pltpu.SemaphoreType.DMA((COPIES,)),
             pltpu.SemaphoreType.DMA((COPIES,)),
         ],

time: 102 us -> 97.4 us (0.955)
  Pallas kernels: 100 us -> 95.7 us
    pallas_call x1, Pallas kernels: 100 us -> 95.7 us  [body(): pl.pallas_call(layer_kernel, out_shape=pltpu.VMEM((TOK, D), BF16), in_spe...]
where the time goes in v3:
time: 97.4 us; the launch traced here: 96.4 us
  Pallas kernels  95.7 us (98%)
    pallas_call x1, Pallas kernels, body(): pl.pallas_call(layer_kernel, out_shape=pltpu.VMEM((TOK, D), BF16), in_spe...  95.7 us

profile of v3, /device:TPU:4, one launch (start us, length us, event | category | flops | bytes accessed | tf_op | source)
XLA Modules:
  0.0 96.4 jit_solution(6356679091126930609)
XLA Ops:
  0.0 95.7 %moe_layer.1 = bf16[128,1024]{1,0:T(8,128)(2,1)S(1)} custom-call(bf16[128,1024]{1,0:T(8,128)(2,1)} %tokens.1, s32[2,128]{1,0:T(2,128)} %bitcast.13, f32[1,1024]{1,0:T(1,128)} %bitcast.11, bf16[8,1024]{1,0:T(8,128)(2,1)} %bitcast.10, f32[1,1024]{1,0:T(1,128)} %bitcast.12, bf16[1024,128]{1,0:T(8,128)(2,1)} %bitcast.7, bf16[1024,128]{1,0:T(8,128)(2,1)} %bitcast.8, ...), custom_call_target="tpu_custom_call" | custom-call | tf_op jit(solution)/shard_map/moe_layer/pallas_call | solution.py:515
  95.7 0.7 copy.13

commit v4 on v3

--- a/solution.py
+++ b/solution.py
@@ -20,8 +20,6 @@
 WIDTHS = (256, 256, 256, 256)
 NC = len(WIDTHS)
 COLUMNS = tuple(pl.ds(sum(WIDTHS[:c]), WIDTHS[c]) for c in range(NC))
-PARTS = [(columns,) for columns in COLUMNS[:-1]]
-PARTS.append(tuple(pl.ds(D - WIDTHS[-1] + at, WIDTHS[-1] // 2) for at in (0, WIDTHS[-1] // 2)))
 OTHERS = pl.ds(WIDTHS[0], D - WIDTHS[0])
 OPP, MATE, SWAP, OWN = range(YN)
 HALF_R = ROWS // 2
@@ -64,12 +62,12 @@
 
 
 STEPS = (
-    5, 0, 3, 2, 7, 67, 98, 4, 10, 6, 42, 8, 68, 40, 15, 12, 11, 13, 33, 41, 73, 76, 90, 1, 53, 19, 69, 55, 54, 72, 14,
-    46, 56, 16, 27, 85, 39, 9, 81, 99, 57, 18, 77, 22, 37, 21, 45, 17, 20, 44, 86, 70, 31, 58, 30, 80, 59, 25, 74, 61,
-    32, 34, 28, 38, 60, 43, 48, 82, 36, 78, 87, 24, 26, 23, 35, 75, 107, 71, 50, 91, 47, 83, 106, 105, 63, 62, 64,
-    109, 103, 94, 49, 108, 65, 100, 95, 92, 104, 88, 79, 84, 52, 51, 66, 110, 111, 96, 101, 112, 89, 93, 113, 120,
-    114, 97, 102, 121, 122, 129, 130, 131, 115, 123, 138, 139, 147, 124, 140, 29, 133, 132, 116, 148, 149, 141, 125,
-    142, 117, 118, 134, 150, 143, 119, 127, 136, 126, 135, 151, 152, 144, 145, 128, 153, 137, 146,
+    3, 0, 2, 7, 5, 10, 76, 98, 85, 90, 4, 15, 41, 67, 12, 42, 13, 6, 11, 33, 8, 1, 39, 40, 14, 27, 54, 53, 22, 37, 21,
+    56, 80, 28, 29, 45, 16, 23, 19, 9, 91, 72, 68, 30, 34, 81, 86, 25, 43, 55, 57, 38, 58, 18, 24, 31, 35, 20, 77, 44,
+    46, 59, 73, 36, 17, 82, 60, 69, 87, 26, 50, 61, 74, 32, 104, 70, 99, 83, 103, 63, 64, 78, 107, 49, 47, 65, 62, 48,
+    109, 105, 75, 100, 71, 94, 95, 108, 106, 88, 79, 52, 92, 66, 84, 51, 110, 112, 111, 114, 113, 96, 101, 93, 89,
+    115, 121, 122, 97, 102, 123, 130, 124, 131, 132, 139, 116, 140, 141, 133, 125, 142, 134, 117, 143, 126, 135, 127,
+    128, 144, 137, 136, 118, 119, 145, 146, 120, 129, 138, 147,
 )
 
 
@@ -210,14 +208,13 @@
         add(("pf", c), "c", psend.at[OPP, :, cols], precv.at[OPP, :, cols], partner)
         rest = pl.ds(MATE, 3)
         add(("pn", c), "c", psend.at[rest, :, cols], precv.at[rest, :, cols], partner)
-        for p, cols in enumerate(PARTS[c]):
-            add(("y1", c, p), "y", y1s.at[:, cols], y1r.at[:, cols], mate)
-            add(("y2", c, p), "y", y2s.at[:, cols], y2r.at[:, cols], mate)
-            add(("y3", c, p), "s", y3s.at[:, cols], y3r.at[:, cols], swap)
-            for way in range(2):
-                add(("x1", way, c, p), f"x{way}", xs1.at[way, :, cols], xr1.at[way, :, cols], to_x[way])
-                add(("x2", way, c, p), f"x{way}", xs2.at[way, :, cols], xr2.at[way, :, cols], to_x[way])
-                add(("x3", way, c, p), f"x{way}", xs3.at[way, :, cols], xr3.at[way, :, cols], to_x[way])
+        add(("y1", c), "y", y1s.at[:, cols], y1r.at[:, cols], mate)
+        add(("y2", c), "y", y2s.at[:, cols], y2r.at[:, cols], mate)
+        add(("y3", c), "s", y3s.at[:, cols], y3r.at[:, cols], swap)
+        for way in range(2):
+            add(("x1", way, c), f"x{way}", xs1.at[way, :, cols], xr1.at[way, :, cols], to_x[way])
+            add(("x2", way, c), f"x{way}", xs2.at[way, :, cols], xr2.at[way, :, cols], to_x[way])
+            add(("x3", way, c), f"x{way}", xs3.at[way, :, cols], xr3.at[way, :, cols], to_x[way])
     assert len(links.copies) <= COPIES
 
     row_iota = lax.broadcasted_iota(jnp.int32, (TOK, TOK), 0)
@@ -368,12 +365,19 @@
     def gate_up(s):
         @step(1.0, 30, f"gate_up_{s}", every_row, of_slot[s] + rows_here)
         def _():
-            for k in range(YN):
-                both = dot(rows[k].reshape(ROWS, D), gu[s])
-                hid[pl.ds(k * ROWS, ROWS), pl.ds(s * HID, HID)] = silu_mul(both[:, :HID], both[:, HID:])
+            products(s, (OPP,) if s == 4 else range(YN))
+
+    def products(s, positions):
+        for k in positions:
+            both = dot(rows[k].reshape(ROWS, D), gu[s])
+            hid[pl.ds(k * ROWS, ROWS), pl.ds(s * HID, HID)] = silu_mul(both[:, :HID], both[:, HID:])
 
     for s in (0, 1, 7, 2, 6, 3, 5, 4):
         gate_up(s)
+    @step(0.8, 23, "gate_up_rest", [], ["gate_up_4", "far_0"])
+    def _():
+        products(4, (MATE, SWAP, OWN))
+
     hidden_done = [f"gate_up_{s}" for s in range(ZN)]
 
     def way_back(c):
@@ -387,37 +391,34 @@
                 pown[first + k, :, columns] = part[k * ROWS : k * ROWS + HALF_R]
                 psend[first + k, :, columns] = part[k * ROWS + HALF_R : (k + 1) * ROWS].astype(BF16)
 
-        @step(0.6, 24, f"far_{c}", needs, hidden_done + ["own_down_n", "own_down_f"], [("pf", c)])
-        def _():
-            down_out(OPP, 1)
-
-        @step(1.4, 25, f"near_{c}", [], [f"far_{c}"], [("pn", c)])
-        def _():
-            down_out(MATE, 3)
-
-    def home(c, p):
-        columns = PARTS[c][p]
-
         def chip(pos):
             return pown[pos, :, columns] + precv[pos, :, columns].astype(F32)
 
-        @step(0.1, 9, f"opp_{c}_{p}", [("pf", c)], [f"near_{c}"], [("y1", c, p)])
+        @step(0.6, 24, f"far_{c}", needs, hidden_done + ["own_down_n", "own_down_f"], [("pf", c)])
+        def _():
+            down_out(OPP, 1)
+
+        @step(1.4, 25, f"near_{c}", [], [f"far_{c}", "gate_up_rest"], [("pn", c)])
+        def _():
+            down_out(MATE, 3)
+
+        @step(0.1, 9, f"opp_{c}", [("pf", c)], [f"far_{c}"], [("y1", c)])
         def _():
             y1s[:, columns] = chip(OPP).astype(BF16)
 
-        @step(0.1, 9, f"mate_{c}_{p}", [("pn", c)], [f"near_{c}"], [("y2", c, p)])
+        @step(0.1, 9, f"mate_{c}", [("pn", c)], [f"near_{c}"], [("y2", c)])
         def _():
             y2s[:, columns] = chip(MATE).astype(BF16)
 
-        @step(0.1, 8, f"swap_{c}_{p}", [("y1", c, p), ("pn", c)], [f"near_{c}"], [("y3", c, p)])
+        @step(0.1, 8, f"swap_{c}", [("y1", c), ("pn", c)], [f"near_{c}"], [("y3", c)])
         def _():
             y3s[:, columns] = (chip(SWAP) + y1r[:, columns].astype(F32)).astype(BF16)
 
         @step(
-            0.45, 8, f"combine_{c}_{p}",
-            [("y2", c, p), ("y3", c, p), ("pn", c)] + [("sc", rx) for rx in range(XN)],
+            0.45, 8, f"combine_{c}",
+            [("y2", c), ("y3", c), ("pn", c)] + [("sc", rx) for rx in range(XN)],
             [f"near_{c}"] + [f"shared_{rx}" for rx in range(XN)],
-            [("x1", 0, c, p), ("x1", 1, c, p), ("x2", 0, c, p), ("x2", 1, c, p)],
+            [("x1", 0, c), ("x1", 1, c), ("x2", 0, c), ("x2", 1, c)],
         )
         def _():
             rrow[:, columns] = (chip(OWN) + y2r[:, columns].astype(F32)).astype(BF16)
@@ -440,7 +441,7 @@
             cown[:, columns] = part(0)
 
         def x_merge(way):
-            @step(0.06, 7, f"x_merge_{way}_{c}_{p}", [("x1", way, c, p)], [f"combine_{c}_{p}"], [("x3", way, c, p)])
+            @step(0.06, 7, f"x_merge_{way}_{c}", [("x1", way, c)], [f"combine_{c}"], [("x3", way, c)])
             def _():
                 xs3[way, :, columns] = (
                     xmerge[way, :, columns] + xr1[way, :, columns].astype(F32)
@@ -449,7 +450,7 @@
         x_merge(0)
         x_merge(1)
 
-        @step(0.1, 12, f"finish_{c}_{p}", [(k, way, c, p) for k in ("x2", "x3") for way in range(2)], [f"combine_{c}_{p}"])
+        @step(0.1, 12, f"finish_{c}", [(k, way, c) for k in ("x2", "x3") for way in range(2)], [f"combine_{c}"])
         def _():
             own = cown[:, columns]
             out[pl.ds(0, HALF_T), columns] = (
@@ -461,8 +462,6 @@
 
     for c in range(NC):
         way_back(c)
-        for p in range(len(PARTS[c])):
-            home(c, p)
 
     only = {"n": native, "f": foreign}
     for name in plan.order():

time: 97.4 us -> 98.8 us (1.014)
  Pallas kernels: 95.7 us -> 97.2 us
    pallas_call x1, Pallas kernels: 95.7 us -> 97.2 us  [body(): pl.pallas_call(layer_kernel, out_shape=pltpu.VMEM((TOK, D), BF16), in_spe...]
where the time goes in v4:
time: 98.8 us; the launch traced here: 97.9 us
  Pallas kernels  97.2 us (98%)
    pallas_call x1, Pallas kernels, body(): pl.pallas_call(layer_kernel, out_shape=pltpu.VMEM((TOK, D), BF16), in_spe...  97.2 us

profile of v4, /device:TPU:4, one launch (start us, length us, event | category | flops | bytes accessed | tf_op | source)
XLA Modules:
  0.0 97.9 jit_solution(1733160221737422618)
XLA Ops:
  0.0 97.2 %moe_layer.1 = bf16[128,1024]{1,0:T(8,128)(2,1)S(1)} custom-call(bf16[128,1024]{1,0:T(8,128)(2,1)} %tokens.1, s32[2,128]{1,0:T(2,128)} %bitcast.13, f32[1,1024]{1,0:T(1,128)} %bitcast.11, bf16[8,1024]{1,0:T(8,128)(2,1)} %bitcast.10, f32[1,1024]{1,0:T(1,128)} %bitcast.12, bf16[1024,128]{1,0:T(8,128)(2,1)} %bitcast.7, bf16[1024,128]{1,0:T(8,128)(2,1)} %bitcast.8, ...), custom_call_target="tpu_custom_call" | custom-call | tf_op jit(solution)/shard_map/moe_layer/pallas_call | solution.py:514
  97.2 0.7 copy.13
